TPU v7x, 32 devices: a whole 2x2x4 slice. The times are simulated.
32 devices in a mesh: rep: 2 (over y), gx: 16 (over z, x, core).
Axes of the slice: x: 2, y: 2, z: 4, core: 2. Of those that a mesh axis runs over, the one named last changes fastest.
Arguments:
- positions: float32 [3, 32768], P(None, ('rep', 'gx')), parts along dimension 1, may hold values from 0 to 8, as said below
- field: float32 [3, 32768], P(None, ('rep', 'gx')), parts along dimension 1, may hold values from -45 to 45
- inv_polar: float32 [32768], P(('rep', 'gx')), parts along dimension 0, may hold values from 2 to 8
- x_spline: float32 [2, 5, 32768], P(None, None, ('rep', 'gx')), parts along dimension 2, may hold values from -1 to 1, as said below
- yz_spline: float32 [4, 32768, 128], P(None, ('rep', 'gx')), parts along dimension 1, may hold values from -1 to 1, as said below
- tile_list: int32 [256, 7], P(('rep', 'gx')), parts along dimension 0, may hold values from 0 to 13, as said below
- tile_count: int32 [256], P(('rep', 'gx')), parts along dimension 0, may hold values from 1 to 7, as said below
Outputs:
- dipoles: float32 [3, 32768], P(None, ('rep', 'gx')), parts along dimension 1
- residual: float32 [3, 32768], P(None, ('rep', 'gx')), parts along dimension 1
There are 2 independent parts, one for each index of `rep`. A program takes and returns all parts, laid end to end along the dimension named above; each array names one. Nothing has to cross between parts.
Inputs may be any that keep to these rules, and one draw needn't show every extreme that they name: `positions`: the first coordinate of an atom of block b of its slab lies in [b, b + 1); the other two lie in [0, 2). x_spline[0, k, i] and x_spline[1, k, i] are the cardinal B-spline of order 5 and its derivative at u_i + 4 - k for some u_i in [0, 1). `yz_spline`: rows 0 and 1 hold, for each atom, the cardinal B-spline of order 5 and its derivative at u + 4 - k placed at grid line (t + k) mod 128 for k < 5, for some start t and some u in [0, 1), and zero elsewhere; rows 2 and 3 likewise with their own start and offset. `tile_list`: row g = s * 8 + b lists in rising order the extended blocks b + 3 + e, -3 <= e <= 3, for which global blocks g and g + e (modulo 128) are neighbours; being neighbours is symmetric and always holds for e = 0; entries from tile_count[g] on equal b + 3. `tile_count`: global block 0 has all 7 neighbours.
All inputs are finite; a program needn't handle non-finite values.
Results may differ from a plain program's by a relative error of at most 0.0003.
Values sent between devices are 32-bit elements; how exact they have to be, the bound alone decides.
No kernel may reach another device: no remote copies, remote signals or barrier semaphores. Data moves between devices by JAX's collectives and lax.ppermute only.
A program may use at most 64 MiB of HBM per device.

v0:
```python
import jax
import numpy as np
import jax.numpy as jnp
from jax import lax
from jax.experimental import pallas as pl
from jax.experimental.pallas import tpu as pltpu
from jax.sharding import PartitionSpec as P

GRID = 128
ORDER = 5
TILE = 128
HALO_BLK = 3
ITERS = 3


PAIR_C = 0.025
RECIP_C = 8192.0
DAMP = 0.0008
EXACT = lax.Precision.HIGHEST


def extended(x, sides, width):
    for axis, dim in sides:
        devices, length = (lax.axis_size(axis), x.shape[dim])
        up = [(i, (i + 1) % devices) for i in range(devices)]
        down = [(j, i) for i, j in up]
        last = lax.slice_in_dim(x, length - width, length, axis=dim)
        first = lax.slice_in_dim(x, 0, width, axis=dim)
        before = lax.ppermute(last, axis, up)
        after = lax.ppermute(first, axis, down)
        x = jnp.concatenate([before, x, after], axis=dim)
    return x


def pair_field(home_pos, ext_pos, ext_vec, tile_rows, live_counts):
    slab_blocks = home_pos.shape[1] // TILE
    ext_blocks = ext_pos.shape[1] // TILE
    home_blocks = home_pos.reshape(3, slab_blocks, TILE).transpose(1, 0, 2)
    pos_blocks = ext_pos.reshape(3, ext_blocks, TILE)
    vec_blocks = ext_vec.reshape(3, ext_blocks, TILE)
    slot_index = jnp.arange(tile_rows.shape[1], dtype=jnp.int32)
    self_pair = jnp.eye(TILE, dtype=bool)

    def one_block(carried, scan_item):
        home_block, tile_row, live_count, block_index = scan_item
        near_pos = jnp.take(pos_blocks, tile_row, axis=1)
        near_vec = jnp.take(vec_blocks, tile_row, axis=1)
        offsets = home_block[:, None, :, None] - near_pos[:, :, None, :]
        distance_sq = jnp.sum(offsets * offsets, axis=0) + 1.0
        inverse = lax.rsqrt(distance_sq)
        third_power = inverse * inverse * inverse
        fifth_power = third_power * inverse * inverse
        same_block = (tile_row == block_index + HALO_BLK)[:, None, None]
        live_mask = (slot_index < live_count)[:, None, None] & ~(same_block & self_pair[None])
        third_power = jnp.where(live_mask, third_power, 0.0)
        fifth_power = jnp.where(live_mask, fifth_power, 0.0)
        projection = jnp.sum(offsets * near_vec[:, :, None, :], axis=0)
        field_sum = jnp.sum(
            third_power[None] * near_vec[:, :, None, :]
            - 3.0 * (fifth_power * projection)[None] * offsets,
            axis=(1, 3),
        )
        return (carried, PAIR_C * field_sum)

    block_ids = jnp.arange(slab_blocks, dtype=jnp.int32)
    unused_carry, blocks_out = lax.scan(
        one_block, jnp.zeros((), jnp.float32), (home_blocks, tile_rows, live_counts, block_ids)
    )
    return blocks_out.transpose(1, 0, 2).reshape(3, slab_blocks * TILE)


def slab_weights(local_plane, x_spline, planes):
    spline_steps = jnp.arange(ORDER, dtype=jnp.int32)
    plane_index = jnp.arange(planes, dtype=jnp.int32)
    matches = local_plane[None, :, None] + spline_steps[:, None, None] == plane_index[None, None, :]
    spline_value = jnp.sum(jnp.where(matches, x_spline[0][:, :, None], 0.0), axis=0)
    spline_slope = jnp.sum(jnp.where(matches, x_spline[1][:, :, None], 0.0), axis=0)
    return (spline_value, spline_slope)


def spread_dipoles(vector, spline_value, spline_slope, yz_spline):
    atoms_here = spline_value.shape[0]
    planes = spline_value.shape[1]
    grid_lines = yz_spline.shape[2]
    lead_terms = (vector[0][:, None] * spline_slope)[:, :, None] * yz_spline[0][:, None, :]
    lead_terms = (
        lead_terms + (vector[1][:, None] * spline_value)[:, :, None] * yz_spline[1][:, None, :]
    )
    tail_terms = (vector[2][:, None] * spline_value)[:, :, None] * yz_spline[0][:, None, :]
    contract = (((0,), (0,)), ((), ()))
    charge = lax.dot_general(
        lead_terms.reshape(atoms_here, planes * grid_lines), yz_spline[2], contract, precision=EXACT
    )
    charge = charge + lax.dot_general(
        tail_terms.reshape(atoms_here, planes * grid_lines), yz_spline[3], contract, precision=EXACT
    )
    return charge.reshape(planes, grid_lines, grid_lines)


def gather_field(potential, spline_value, spline_slope, yz_spline):
    planes = potential.shape[0]
    grid_lines = potential.shape[1]
    atoms_here = spline_value.shape[0]
    flat_grid = potential.reshape(planes * grid_lines, grid_lines)
    contract = (((1,), (1,)), ((), ()))
    plain_sum = lax.dot_general(yz_spline[2], flat_grid, contract, precision=EXACT).reshape(
        atoms_here, planes, grid_lines
    )
    tilted_sum = lax.dot_general(yz_spline[3], flat_grid, contract, precision=EXACT).reshape(
        atoms_here, planes, grid_lines
    )
    first_comp = jnp.sum(
        spline_slope[:, :, None] * yz_spline[0][:, None, :] * plain_sum, axis=(1, 2)
    )
    second_comp = jnp.sum(
        spline_value[:, :, None] * yz_spline[1][:, None, :] * plain_sum, axis=(1, 2)
    )
    third_comp = jnp.sum(
        spline_value[:, :, None] * yz_spline[0][:, None, :] * tilted_sum, axis=(1, 2)
    )
    return jnp.stack([first_comp, second_comp, third_comp])


def mode_of(freq, size):
    half_size = size // 2
    mode_num = jnp.where(freq <= half_size, freq, freq - half_size)
    weight = jnp.where((freq == 0) | (freq == half_size), 1.0 / size, 2.0 / size)
    return (mode_num.astype(jnp.float32), weight.astype(jnp.float32))


def basis_rows(size, points):
    freq = jnp.arange(size, dtype=jnp.int32)
    half_size = size // 2
    mode_num = jnp.where(freq <= half_size, freq, freq - half_size)
    phase = mode_num[:, None] * points[None, :] % size
    angle = phase.astype(jnp.float32) * (2.0 * jnp.pi / size)
    return jnp.where((freq <= half_size)[:, None], jnp.cos(angle), jnp.sin(angle))


def kernel_block(x_modes, x_weights, y_modes, y_weights, z_modes, z_weights):
    mode_sq = (
        x_modes[:, None, None] * x_modes[:, None, None]
        + y_modes[None, :, None] * y_modes[None, :, None]
        + z_modes[None, None, :] * z_modes[None, None, :]
    )
    safe_sq = jnp.where(mode_sq > 0, mode_sq, 1.0)
    green = jnp.where(mode_sq > 0, RECIP_C * jnp.exp(-DAMP * safe_sq) / safe_sq, 0.0)
    return green * x_weights[:, None, None] * y_weights[None, :, None] * z_weights[None, None, :]


def forward_lines(charge, fourier_rows):
    along_z = jnp.einsum("pyz,kz->pyk", charge, fourier_rows, precision=EXACT)
    return jnp.einsum("jy,pyk->pjk", fourier_rows, along_z, precision=EXACT)


def inverse_lines(spectrum, fourier_rows):
    along_z = jnp.einsum("pjk,kz->pjz", spectrum, fourier_rows, precision=EXACT)
    return jnp.einsum("jy,pjz->pyz", fourier_rows, along_z, precision=EXACT)


def per_device_general(positions, field, inv_polar, x_spline, yz_spline, tile_list, tile_count):
    rank_count = lax.axis_size("gx")
    rank_index = lax.axis_index("gx")
    atoms_here = positions.shape[1]
    planes = GRID // rank_count
    extent = planes + 4
    halo_atoms = HALO_BLK * TILE
    slab_blocks = atoms_here // TILE
    local_plane = jnp.arange(atoms_here, dtype=jnp.int32) * planes // atoms_here
    spline_value, spline_slope = slab_weights(local_plane, x_spline, extent)
    ext_pos = extended(positions, (("gx", 1),), halo_atoms)
    shift_x = jnp.concatenate(
        [
            jnp.full((halo_atoms,), -1.0 * slab_blocks, jnp.float32),
            jnp.zeros((atoms_here,), jnp.float32),
            jnp.full((halo_atoms,), 1.0 * slab_blocks, jnp.float32),
        ]
    )
    ext_pos = ext_pos.at[0].add(shift_x)
    fourier_rows = basis_rows(GRID, jnp.arange(GRID, dtype=jnp.int32))
    ky_count = GRID // rank_count
    all_freq = jnp.arange(GRID, dtype=jnp.int32)
    ky_freq = rank_index * ky_count + jnp.arange(ky_count, dtype=jnp.int32)
    full_modes, full_weights = mode_of(all_freq, GRID)
    ky_modes, ky_weights = mode_of(ky_freq, GRID)
    kernel = kernel_block(full_modes, full_weights, ky_modes, ky_weights, full_modes, full_weights)
    kernel = kernel.reshape(GRID, ky_count * GRID)
    source_rows = jnp.arange(rank_count * extent, dtype=jnp.int32)
    points = (source_rows // extent * planes - 2 + source_rows % extent) % GRID
    across = basis_rows(GRID, points)

    def reciprocal(charge):
        spectrum = forward_lines(charge, fourier_rows)
        pencils = lax.all_to_all(spectrum, "gx", split_axis=1, concat_axis=0, tiled=True)
        rows_in = pencils.shape[0]
        flat_pencils = pencils.reshape(rows_in, ky_count * GRID)
        spectral_lines = jnp.dot(across, flat_pencils, precision=EXACT) * kernel
        returned_lines = lax.dot_general(
            across, spectral_lines, (((0,), (0,)), ((), ())), precision=EXACT
        )
        returned = lax.all_to_all(
            returned_lines.reshape(rows_in, ky_count, GRID),
            "gx",
            split_axis=0,
            concat_axis=1,
            tiled=True,
        )
        return inverse_lines(returned, fourier_rows)

    def apply(vector):
        ext_vec = extended(vector, (("gx", 1),), halo_atoms)
        near_field = pair_field(positions, ext_pos, ext_vec, tile_list, tile_count)
        charge = spread_dipoles(vector, spline_value, spline_slope, yz_spline)
        far_field = gather_field(reciprocal(charge), spline_value, spline_slope, yz_spline)
        return inv_polar[None, :] * vector + far_field - near_field

    def paired(residual, precond, applied):
        return lax.psum((jnp.sum(residual * precond), jnp.sum(applied * precond)), "gx")

    dipoles = jnp.zeros_like(field)
    residual = field
    precond = field / inv_polar[None, :]
    applied = apply(precond)
    rz_now, curvature = paired(residual, precond, applied)
    step_size = rz_now / curvature
    direction = precond
    applied_dir = applied
    for sweep_index in range(ITERS):
        dipoles = dipoles + step_size * direction
        residual = residual - step_size * applied_dir
        if sweep_index + 1 < ITERS:
            precond = residual / inv_polar[None, :]
            applied = apply(precond)
            rz_next, curvature = paired(residual, precond, applied)
            beta_ratio = rz_next / rz_now
            step_size = rz_next / (curvature - beta_ratio * rz_next / step_size)
            direction = precond + beta_ratio * direction
            applied_dir = applied + beta_ratio * applied_dir
            rz_now = rz_next
    return (dipoles, residual)


F32 = jnp.float32
BF16 = jnp.bfloat16
ROWS = 8
SPAN = 2 * HALO_BLK + 1
IN_VMEM = pl.BlockSpec(memory_space=pltpu.VMEM)
IN_SMEM = pl.BlockSpec(memory_space=pltpu.SMEM)
IN_HBM = pl.BlockSpec(memory_space=pl.ANY)
REACH = ORDER - 1
NT = (((1,), (1,)), ((), ()))


def params(flops, vmem=None):
    return dict(
        cost_estimate=pl.CostEstimate(flops=flops, bytes_accessed=4 << 20, transcendentals=0),
        compiler_params=pltpu.CompilerParams(vmem_limit_bytes=vmem) if vmem else None,
    )


def halves(x):
    high = x.astype(BF16).astype(F32)
    return high, x - high


def bdot(a, b):
    return jnp.dot(a, b, preferred_element_type=F32)


def spline_values(u):
    w = 1.0 - u
    u2, w2 = u * u, w * w
    c = 1.0 / 24.0
    return [
        c * (w2 * w2),
        c * (11.0 + u * (-12.0 + u * (-6.0 + u * (12.0 - 4.0 * u)))),
        c * (11.0 + u * (12.0 + u * (-6.0 + u * (-12.0 + 6.0 * u)))),
        c * (1.0 + u * (4.0 + u * (6.0 + u * (4.0 - 4.0 * u)))),
        c * (u2 * u2),
    ]


def spline_slopes(u):
    w = 1.0 - u
    c = 1.0 / 6.0
    return [
        -c * (w * w * w),
        c * (-3.0 + u * (-3.0 + u * (9.0 - 4.0 * u))),
        c * (3.0 + u * (-3.0 + u * (-9.0 + 6.0 * u))),
        c * (1.0 + u * (3.0 + u * (3.0 - 4.0 * u))),
        c * (u * u * u),
    ]


def block_rows(ref, row):
    return jnp.concatenate(
        [ref[row : row + 1, b * TILE : (b + 1) * TILE] for b in range(ref.shape[1] // TILE)], axis=0
    )


def pack_kernel(field_ref, ip_ref, xs_ref, yz_ref, own_ref, inv_ref, out_ref):
    parts = out_ref.shape[0]
    blocks = field_ref.shape[1] // TILE
    grid = yz_ref.shape[2]
    inv = block_rows(ip_ref, 0)
    inv_ref[...] = inv
    tiles = [block_rows(field_ref, c) / inv for c in range(3)]
    for c in range(3):
        own_ref[c * blocks : (c + 1) * blocks, :] = tiles[c]
    tiles.append(sum(float(k) * block_rows(xs_ref, k) for k in range(1, ORDER)) - 1.5)
    line = lax.broadcasted_iota(jnp.int32, (grid, TILE), 0)
    for axis in range(2):
        starts, offsets = [], []
        for b in range(blocks):
            here = slice(b * TILE, (b + 1) * TILE)
            value = yz_ref[2 * axis, here, :].T
            slope = yz_ref[2 * axis + 1, here, :].T
            used = jnp.where((value != 0.0) | (slope != 0.0), 1.0, 0.0)
            first = used * (1.0 - pltpu.roll(used, 1, 0))
            start = jnp.sum(first * line.astype(F32), axis=0, keepdims=True)
            offset = (line - start.astype(jnp.int32)) & (grid - 1)
            starts.append(start)
            offsets.append(jnp.sum(value * offset.astype(F32), axis=0, keepdims=True) - 1.5)
        tiles.append(jnp.concatenate(starts, axis=0))
        tiles.append(jnp.concatenate(offsets, axis=0))
    for d in range(parts):
        for i, tile in enumerate(tiles):
            out_ref[d, i * blocks : (i + 1) * blocks, :] = tile


def pack_call(field, inv_row, xs, yz, parts):
    blocks = field.shape[1] // TILE
    return pl.pallas_call(
        pack_kernel,
        in_specs=[IN_VMEM] * 4,
        out_specs=[IN_VMEM] * 3,
        out_shape=[
            jax.ShapeDtypeStruct((3 * blocks, TILE), F32),
            jax.ShapeDtypeStruct((blocks, TILE), F32),
            jax.ShapeDtypeStruct((parts, 8 * blocks, TILE), F32),
        ],
        name="pack",
        **params(1 << 26),
    )(field, inv_row, xs, yz)


def prep_kernel(atom_ref, rows_ref, turn_ref, tab_ref, yt_ref):
    blocks = tab_ref.shape[0]
    grid = rows_ref.shape[0]
    tile = lambda i: atom_ref[0, i * blocks : (i + 1) * blocks, :]
    high, low = halves(rows_ref[...])
    twice = jnp.concatenate([high, low], axis=0).astype(BF16)
    matrix = jnp.concatenate([twice, twice], axis=1)
    line = lax.broadcasted_iota(jnp.int32, (grid, TILE), 0)
    start_z, u_z = tile(6).astype(jnp.int32), tile(7)
    values, slopes = spline_values(u_z), spline_slopes(u_z)
    spots = [(start_z + k) & (grid - 1) for k in range(ORDER)]
    for b in range(blocks):
        row = slice(b, b + 1)
        dense = jnp.zeros((grid, TILE), F32)
        tilted = dense
        for k in range(ORDER):
            here = line == spots[k][row]
            dense = jnp.where(here, values[k][row], dense)
            tilted = jnp.where(here, slopes[k][row], tilted)
        high, low = halves(jnp.concatenate([dense, tilted], axis=1))
        both = bdot(matrix, jnp.concatenate([high, low], axis=0).astype(BF16))
        high, low = halves(both[:grid] + both[grid:])
        tab_ref[b] = jnp.concatenate([high, low], axis=0).astype(BF16)
    start_y, u_y = tile(4), tile(5)
    values, slopes = spline_values(u_y), spline_slopes(u_y)
    mode, sine = turn_ref[0], turn_ref[1]
    half = float(grid // 2)
    for b in range(blocks):
        row = slice(b, b + 1)
        phase = (mode * start_y[row]).astype(jnp.int32) + grid // 2
        angle = ((phase & (grid - 1)).astype(F32) - half) * (jnp.pi / (4.0 * half))
        sq = angle * angle
        s = angle * (1.0 + sq * (-1.0 / 6 + sq * (1.0 / 120 + sq * (-1.0 / 5040 + sq / 362880))))
        c = 1.0 + sq * (-0.5 + sq * (1.0 / 24 + sq * (-1.0 / 720 + sq / 40320)))
        for _ in range(2):
            s, c = 2.0 * s * c, 1.0 - 2.0 * s * s
        lead = jnp.where(sine > 0.0, s, c)
        side = jnp.where(sine > 0.0, -c, s)
        for i, weights in enumerate((values, slopes)):
            even = weights[0][row] + sum(weights[k][row] * turn_ref[1 + k] for k in range(1, ORDER))
            odd = sum(weights[k][row] * turn_ref[ORDER + k] for k in range(1, ORDER))
            yt_ref[b, i * ROWS : (i + 1) * ROWS, :] = lead * even - side * odd


def prep_call(atoms, rows, turns, blocks):
    parts = atoms.shape[0]
    grid = rows.shape[0]
    return pl.pallas_call(
        prep_kernel,
        grid=(parts,),
        in_specs=[
            pl.BlockSpec((1, 8 * blocks, TILE), lambda s: (s, 0, 0)),
            pl.BlockSpec(rows.shape, lambda s: (0, 0)),
            pl.BlockSpec(turns.shape, lambda s: (0, 0, 0)),
        ],
        out_specs=[
            pl.BlockSpec((blocks, 2 * grid, 2 * TILE), lambda s: (s, 0, 0)),
            pl.BlockSpec((blocks, 2 * ROWS, TILE), lambda s: (s, 0, 0)),
        ],
        out_shape=[
            jax.ShapeDtypeStruct((parts * blocks, 2 * grid, 2 * TILE), BF16),
            jax.ShapeDtypeStruct((parts * blocks, 2 * ROWS, TILE), F32),
        ],
        name="prep",
        **params(1 << 31),
    )(atoms, rows, turns)


def field_kernel(with_sums, v_ref, atom_ref, tab_hbm, yt_ref, rows_ref, cols_ref, kern_ref, *rest):
    if with_sums:
        sums_ref, out_ref, tab, sem, grid_ref = rest
    else:
        out_ref, tab, sem, grid_ref = rest
    parts = out_ref.shape[0]
    grid = rows_ref.shape[0]
    blocks = tab.shape[0] // parts
    width = ROWS * ORDER

    def fetch(s):
        part = pl.ds(s * blocks, blocks)
        return pltpu.make_async_copy(tab_hbm.at[part], tab.at[part], sem.at[s])

    for s in range(parts):
        fetch(s).start()
    grid_ref[...] = jnp.zeros(grid_ref.shape, F32)

    def plane(q):
        return pl.ds(pl.multiple_of(q * ROWS, ROWS), ROWS)

    def x_weights(s):
        u = atom_ref[s, 3 * blocks : 4 * blocks, :]
        return spline_values(u), spline_slopes(u)

    def spread(s, carry):
        fetch(s).wait()
        value, slope = x_weights(s)
        vec = [v_ref[s, c * blocks : (c + 1) * blocks, :] for c in range(3)]
        a0 = [vec[0] * slope[k] for k in range(ORDER)]
        a1 = [vec[1] * value[k] for k in range(ORDER)]
        a2 = [vec[2] * value[k] for k in range(ORDER)]
        sums = [jnp.zeros((ROWS, grid), F32) for _ in range(blocks + REACH)]
        for b in range(blocks):
            g = s * blocks + b
            row = slice(b, b + 1)
            yt, dyt = yt_ref[g, 0:ROWS, :], yt_ref[g, ROWS : 2 * ROWS, :]
            lead = jnp.concatenate([a0[k][row] * yt + a1[k][row] * dyt for k in range(ORDER)], axis=0)
            tail = jnp.concatenate([a2[k][row] * yt for k in range(ORDER)], axis=0)
            high, low = halves(jnp.concatenate([lead, tail], axis=1))
            lhs = jnp.concatenate([high, low], axis=0).astype(BF16)
            out = lax.dot_general(lhs, tab[g], NT, preferred_element_type=F32)
            out = out[:width] + out[width:]
            out = out[:, :grid] + out[:, grid:]
            for k in range(ORDER):
                sums[b + k] = sums[b + k] + out[k * ROWS : (k + 1) * ROWS]
        for j, tile in enumerate(sums):
            grid_ref[plane(s * blocks + j), :] += tile
        return carry

    lax.fori_loop(0, parts, spread, 0)
    side = REACH // 2
    body = slice(side * ROWS, (side + grid) * ROWS)
    left, right = slice(0, side * ROWS), slice((side + grid) * ROWS, (2 * side + grid) * ROWS)
    first = slice(side * ROWS, 2 * side * ROWS)
    last = slice(grid * ROWS, (side + grid) * ROWS)
    grid_ref[last, :] += grid_ref[left, :]
    grid_ref[first, :] += grid_ref[right, :]

    def product(matrix, x):
        mh, ml = halves(matrix)
        xh, xl = halves(x)
        rhs = jnp.concatenate([xh, xl], axis=0).astype(BF16)
        mh, ml = mh.astype(BF16), ml.astype(BF16)
        return bdot(jnp.concatenate([mh, mh], axis=1), rhs) + bdot(
            jnp.concatenate([ml, ml], axis=1), rhs
        )

    def lines(j):
        return pl.ds(side * ROWS + j, grid, stride=ROWS)

    charge = jnp.concatenate([grid_ref[lines(j), :] for j in range(ROWS)], axis=1)
    spectrum = product(rows_ref[...], charge)
    weighted = spectrum * kern_ref[...]
    potential = product(cols_ref[...], weighted)
    for j in range(ROWS):
        grid_ref[lines(j), :] = potential[:, j * grid : (j + 1) * grid]
    grid_ref[left, :] = grid_ref[last, :]
    grid_ref[right, :] = grid_ref[first, :]
    if with_sums:
        energy = jnp.sum(spectrum * weighted)
        row = lax.broadcasted_iota(jnp.int32, sums_ref.shape, 0)
        sums = sums_ref[...] + jnp.where(row == 5, energy, 0.0)
        for d in range(parts):
            out_ref[d, 3 * blocks :, :] = sums

    def gather(s, carry):
        value, slope = x_weights(s)
        pieces = [halves(grid_ref[plane(s * blocks + q), :]) for q in range(blocks + REACH)]
        fields = ([], [], [])
        for b in range(blocks):
            g = s * blocks + b
            row = slice(b, b + 1)
            yt, dyt = yt_ref[g, 0:ROWS, :], yt_ref[g, ROWS : 2 * ROWS, :]
            near = pieces[b : b + ORDER]
            lhs = jnp.concatenate([x[0] for x in near] + [x[1] for x in near], axis=0).astype(BF16)
            out = bdot(jnp.concatenate([lhs, lhs], axis=1), tab[g])
            out = out[:width] + out[width:]
            tiles = [out[k * ROWS : (k + 1) * ROWS] for k in range(ORDER)]
            f0 = sum(slope[k][row] * tiles[k][:, :TILE] for k in range(ORDER))
            f1 = sum(value[k][row] * tiles[k][:, :TILE] for k in range(ORDER))
            f2 = sum(value[k][row] * tiles[k][:, TILE:] for k in range(ORDER))
            for i, part in enumerate((yt * f0, dyt * f1, yt * f2)):
                fields[i].append(jnp.sum(part, axis=0, keepdims=True))
        for i in range(3):
            out_ref[s, i * blocks : (i + 1) * blocks, :] = jnp.concatenate(fields[i], axis=0)
        return carry

    lax.fori_loop(0, parts, gather, 0)


def field_call(vec, atoms, table, yt, rows, cols, kern, sums=None):
    parts = vec.shape[0]
    grid = rows.shape[0]
    blocks = yt.shape[0] // parts
    args = [vec, atoms, table, yt, rows, cols, kern]
    specs = [IN_VMEM, IN_VMEM, IN_HBM] + [IN_VMEM] * 4
    out_rows = 3 * blocks
    if sums is not None:
        args.append(sums)
        specs.append(IN_VMEM)
        out_rows += ROWS
    return pl.pallas_call(
        lambda *refs: field_kernel(sums is not None, *refs),
        in_specs=specs,
        out_specs=IN_VMEM,
        out_shape=jax.ShapeDtypeStruct((parts, out_rows, TILE), F32),
        scratch_shapes=[
            pltpu.VMEM(table.shape, BF16),
            pltpu.SemaphoreType.DMA((parts,)),
            pltpu.VMEM(((grid + REACH) * ROWS, grid), F32),
        ],
        name="field",
        **params(1 << 31, 56 << 20),
    )(*args)


def pair_kernel(wts_ref, rank_ref, left_ref, pos_ref, right_ref, col_ref, vec_ref, out_ref, acc_ref, near_ref):
    blocks = pos_ref.shape[1] // TILE
    ext = blocks + 2 * HALO_BLK
    total = vec_ref.shape[0] * blocks
    chunk = 32
    shift = 1.0 * blocks
    for c in range(3):
        for j in range(ext):
            if j < HALO_BLK:
                row = left_ref[c : c + 1, j * TILE : (j + 1) * TILE] - (shift if c == 0 else 0.0)
            elif j < HALO_BLK + blocks:
                i = j - HALO_BLK
                row = pos_ref[c : c + 1, i * TILE : (i + 1) * TILE]
            else:
                i = j - HALO_BLK - blocks
                row = right_ref[c : c + 1, i * TILE : (i + 1) * TILE] + (shift if c == 0 else 0.0)
            near_ref[j, c : c + 1, :] = row
            g = lax.rem(rank_ref[0] * blocks + (j - HALO_BLK) + total, total)
            src = lax.div(g, blocks)
            near_ref[j, 3 + c : 4 + c, :] = vec_ref[src, pl.ds(c * blocks + g - src * blocks, 1), :]

    def one_block(b, carry):
        for c in range(TILE // chunk):
            home = col_ref[pl.ds(pl.multiple_of(b * TILE + c * chunk, chunk), chunk), :]
            shape = (chunk, TILE)
            hx = jnp.broadcast_to(home[:, 0:1], shape)
            hy = jnp.broadcast_to(home[:, 1:2], shape)
            hz = jnp.broadcast_to(home[:, 2:3], shape)
            sx = sy = sz = jnp.zeros(shape, F32)
            for e in range(SPAN):
                near = near_ref[b + e]
                dx, dy, dz = hx - near[0:1], hy - near[1:2], hz - near[2:3]
                vx, vy, vz = near[3:4], near[4:5], near[5:6]
                inverse = lax.rsqrt(dx * dx + dy * dy + dz * dz + 1.0)
                square = inverse * inverse
                third = wts_ref[b * SPAN + e] * (inverse * square)
                if e == HALO_BLK:
                    row = lax.broadcasted_iota(jnp.int32, shape, 0) + c * chunk
                    lane = lax.broadcasted_iota(jnp.int32, shape, 1)
                    third = jnp.where(row == lane, 0.0, third)
                fifth = 3.0 * (third * square) * (dx * vx + dy * vy + dz * vz)
                sx = sx + (third * vx - fifth * dx)
                sy = sy + (third * vy - fifth * dy)
                sz = sz + (third * vz - fifth * dz)
            acc_ref[0, pl.ds(c * chunk, chunk), :] = sx
            acc_ref[1, pl.ds(c * chunk, chunk), :] = sy
            acc_ref[2, pl.ds(c * chunk, chunk), :] = sz
        for i in range(3):
            out_ref[pl.ds(i * blocks + b, 1), :] = PAIR_C * jnp.sum(acc_ref[i].T, axis=0, keepdims=True)
        return carry

    lax.fori_loop(0, blocks, one_block, 0)


def pair_call(wts, rank, left, pos, right, cols, vec):
    blocks = pos.shape[1] // TILE
    return pl.pallas_call(
        pair_kernel,
        in_specs=[IN_SMEM, IN_SMEM] + [IN_VMEM] * 5,
        out_specs=IN_VMEM,
        out_shape=jax.ShapeDtypeStruct((3 * blocks, TILE), F32),
        scratch_shapes=[
            pltpu.VMEM((3, TILE, TILE), F32),
            pltpu.VMEM((blocks + 2 * HALO_BLK, ROWS, TILE), F32),
        ],
        name="pair",
        **params(1 << 30),
    )(wts, rank, left, pos, right, cols, vec)


def update_kernel(ret_ref, pair_ref, inv_ref, own_ref, out_ref):
    blocks = inv_ref.shape[0]
    far = jnp.sum(ret_ref[...], axis=0) - pair_ref[...]
    inv = inv_ref[...]
    vec = jnp.concatenate([far[c * blocks : (c + 1) * blocks] / inv for c in range(3)], axis=0)
    own_ref[...] = vec
    for d in range(out_ref.shape[0]):
        out_ref[d] = vec


def update_call(returned, pair, inv):
    parts = returned.shape[0]
    return pl.pallas_call(
        update_kernel,
        in_specs=[IN_VMEM] * 3,
        out_specs=[IN_VMEM] * 2,
        out_shape=[
            jax.ShapeDtypeStruct(pair.shape, F32),
            jax.ShapeDtypeStruct((parts,) + pair.shape, F32),
        ],
        name="update",
        **params(1 << 24),
    )(returned, pair, inv)


def moments_kernel(v0_ref, v1_ref, v2_ref, inv_ref, pair_ref, out_ref):
    ip = jnp.concatenate([inv_ref[...]] * 3, axis=0)
    v0, v1, v2 = v0_ref[...], v1_ref[...], v2_ref[...]
    d1, d2 = ip * v1, ip * v2
    terms = (v0 * (ip * v0), v0 * d1, v1 * d1, v1 * d2, v2 * d2, -(v2 * pair_ref[...]))
    row = lax.broadcasted_iota(jnp.int32, out_ref.shape, 0)
    sums = jnp.zeros(out_ref.shape, F32)
    for k, term in enumerate(terms):
        sums = sums + jnp.where(row == k, jnp.sum(term), 0.0)
    out_ref[...] = sums


def moments_call(vectors, inv, pair):
    return pl.pallas_call(
        moments_kernel,
        in_specs=[IN_VMEM] * 5,
        out_specs=IN_VMEM,
        out_shape=jax.ShapeDtypeStruct((ROWS, TILE), F32),
        name="moments",
        **params(1 << 24),
    )(*vectors, inv, pair)


def finish_kernel(ret_ref, pair_ref, v0_ref, v1_ref, v2_ref, inv_ref, dip_ref, res_ref):
    blocks = inv_ref.shape[0]
    summed = jnp.sum(ret_ref[...], axis=0)
    total = summed[3 * blocks :]
    h = summed[: 3 * blocks] - pair_ref[...]
    m = [total[k : k + 1, 0:1] for k in range(6)]
    s = [lax.rsqrt(m[2 * i]) for i in range(3)]
    g = [[m[i + j] * s[i] * s[j] for j in range(3)] for i in range(3)]
    b = [-m[i + 3] * s[i] for i in range(3)]
    l10 = g[1][0] / g[0][0]
    l20 = g[2][0] / g[0][0]
    p11 = g[1][1] - l10 * g[0][1]
    p12 = g[1][2] - l10 * g[0][2]
    l21 = p12 / p11
    p22 = g[2][2] - l20 * g[0][2] - l21 * p12
    b1 = b[1] - l10 * b[0]
    b2 = b[2] - l20 * b[0] - l21 * b1
    y2 = b2 / p22
    y1 = (b1 - p12 * y2) / p11
    y0 = (b[0] - g[0][1] * y1 - g[0][2] * y2) / g[0][0]
    a0, a1, a2 = s[0] * y0, s[1] * y1, s[2] * y2
    scale = 1.0 / (a0 - a1 + a2 - 1.0)
    a0, a1, a2, a3 = a0 * scale, a1 * scale, a2 * scale, scale
    c2 = -a3
    c1 = a3 - a2
    c0 = a2 - a3 - a1
    ip = jnp.concatenate([inv_ref[...]] * 3, axis=0)
    v0, v1, v2 = v0_ref[...], v1_ref[...], v2_ref[...]
    dip = c0 * v0 + c1 * v1 + c2 * v2
    res = ip * (a0 * v0 + a1 * v1 + a2 * v2) + a3 * h
    for c in range(3):
        for b in range(blocks):
            row = slice(c * blocks + b, c * blocks + b + 1)
            here = slice(b * TILE, (b + 1) * TILE)
            dip_ref[c : c + 1, here] = dip[row]
            res_ref[c : c + 1, here] = res[row]


def finish_call(returned, pair, vectors, inv):
    atoms = inv.shape[0] * TILE
    return pl.pallas_call(
        finish_kernel,
        in_specs=[IN_VMEM] * 6,
        out_specs=[IN_VMEM] * 2,
        out_shape=[jax.ShapeDtypeStruct((3, atoms), F32)] * 2,
        name="finish",
        **params(1 << 24),
    )(returned, pair, *vectors, inv)


def fourier_matrix(size):
    freq = np.arange(size)
    mode = np.where(freq <= size // 2, freq, freq - size // 2)
    angle = (mode[:, None] * np.arange(size)[None, :] % size) * (2.0 * np.pi / size)
    rows = np.where((freq <= size // 2)[:, None], np.cos(angle), np.sin(angle))
    return rows.astype(np.float32)


def swap(x):
    return lax.all_to_all(x, "gx", split_axis=0, concat_axis=0, tiled=True)


def per_device_modes(positions, field, inv_polar, x_spline, yz_spline, tile_list, tile_count):
    parts = lax.axis_size("gx")
    rank = lax.axis_index("gx")
    atoms = positions.shape[1]
    halo = HALO_BLK * TILE
    blocks = atoms // TILE
    up = [(i, (i + 1) % parts) for i in range(parts)]
    down = [(j, i) for i, j in up]

    own, inv, packed = pack_call(
        field, inv_polar[None, :], x_spline.reshape(2 * ORDER, atoms), yz_spline, parts
    )
    everyone = swap(packed)
    left = lax.ppermute(positions[:, atoms - halo :], "gx", up)
    right = lax.ppermute(positions[:, :halo], "gx", down)
    home_cols = jnp.pad(positions, ((0, ROWS - 3), (0, 0))).T

    offsets = jnp.arange(SPAN, dtype=jnp.int32)
    block_ids = jnp.arange(blocks, dtype=jnp.int32)
    live = jnp.arange(tile_list.shape[1], dtype=jnp.int32)[None, :] < tile_count[:, None]
    hit = tile_list[:, :, None] == block_ids[:, None, None] + offsets[None, None, :]
    wts = jnp.sum((hit & live[:, :, None]).astype(F32), axis=1).reshape(-1)

    matrix = fourier_matrix(GRID)
    rows, cols = jnp.asarray(matrix), jnp.asarray(matrix.T)
    all_freq = jnp.arange(GRID, dtype=jnp.int32)
    ky_count = GRID // parts
    ky_freq = rank * ky_count + jnp.arange(ky_count, dtype=jnp.int32)
    full_modes, full_weights = mode_of(all_freq, GRID)
    ky_modes, ky_weights = mode_of(ky_freq, GRID)
    kern = kernel_block(full_modes, full_weights, ky_modes, ky_weights, full_modes, full_weights)
    kern = kern.reshape(GRID, ky_count * GRID)
    steps = jnp.arange(1, ORDER).astype(F32)
    angle = steps[:, None] * ky_modes[None, :] * (2.0 * jnp.pi / GRID)
    sine = (ky_freq > GRID // 2).astype(F32)
    turns = jnp.concatenate([ky_modes[None], sine[None], jnp.cos(angle), jnp.sin(angle)])
    turns = jnp.broadcast_to(turns[:, :, None], turns.shape + (TILE,))

    table, yt = prep_call(everyone, rows, turns, blocks)
    vec, vectors = everyone, [own]
    rank_id = rank[None].astype(jnp.int32)
    for step in range(ITERS):
        last = step + 1 == ITERS
        pair = pair_call(wts, rank_id, left, positions, right, home_cols, vec)
        sums = moments_call(vectors, inv, pair) if last else None
        returned = swap(field_call(vec, everyone, table, yt, rows, cols, kern, sums))
        if not last:
            own, packed = update_call(returned, pair, inv)
            vectors.append(own)
            vec = swap(packed)
    dipoles, residual = finish_call(returned, pair, vectors, inv)
    return (dipoles, residual)


def per_device(positions, *others):
    parts = lax.axis_size("gx")
    atoms = positions.shape[1]
    planes = GRID // parts
    modes = (
        parts * ROWS == GRID
        and atoms == planes * TILE
        and planes == ROWS
        and atoms >= HALO_BLK * TILE
        and ORDER == 5
        and ITERS == 3
    )
    run = per_device_modes if modes else per_device_general
    return run(positions, *others)


def solution(mesh):
    placed = (
        P(None, ("rep", "gx")),
        P(None, ("rep", "gx")),
        P(("rep", "gx")),
        P(None, None, ("rep", "gx")),
        P(None, ("rep", "gx"), None),
        P(("rep", "gx"), None),
        P(("rep", "gx")),
    )
    return jax.shard_map(
        per_device,
        mesh=mesh,
        in_specs=placed,
        out_specs=(P(None, ("rep", "gx")), P(None, ("rep", "gx"))),
        check_vma=False,
    )
```

profile of v0, /device:TPU:0, one launch (start us, length us, event | category | flops | bytes accessed | tf_op | source)
XLA Modules:
  0.0 184.5 jit_solution(6528431079015456567)
XLA Ops:
  1.4 5.4 %collective-permute-start.1 = (f32[3,384]{1,0:T(4,128)S(1)}, f32[3,384]{1,0:T(4,128)S(1)}, u32[]{:S(2)}, u32[]{:S(2)}) collective-permute-start(f32[3,384]{1,0:T(4,128)S(1)} %get-tuple-element.20), channel_id=1, source_target_pairs={{1,0},{2,1},{3,2},{4,3},{5,4},{6,5},{7,6},{8,7},{9,8},{10,9},{11,1... | collective-permute-start | bytes 13832 | tf_op jit(solution)/shard_map/ppermute | solution.py:746
  6.8 0.8 copy.15
  8.3 3.2 %pack.1 = (f32[24,128]{1,0:T(8,128)}, f32[8,128]{1,0:T(8,128)}, f32[16,64,128]{2,1,0:T(8,128)}) custom-call(f32[3,1024]{1,0:T(4,128)} %field_ref.1, f32[1,1024]{1,0:T(1,128)} %bitcast.16, f32[10,1024]{1,0:T(8,128)} %reshape.170.xs_ref, f32[4,1024,128]{2,1,0:T(8,128)} %yz_ref.1), custom_call_target="tpu_custom_call" | custom-call | flops 67108864 | bytes 4194304 | tf_op jit(solution)/shard_map/pack/pallas_call | solution.py:333
  11.5 5.8 %all-to-all-start = ((f32[16,64,128]{2,1,0:T(8,128)}), f32[16,64,128]{2,1,0:T(8,128)S(1)}, u32[]{:S(2)}, u32[]{:S(2)}) async-start(f32[16,64,128]{2,1,0:T(8,128)} %get-tuple-element.11), calls=%async_computation | async-start | bytes 1048576 | tf_op jit(solution)/shard_map/all_to_all | solution.py:729
  18.5 1.1 fusion.2.refs_6_
  19.6 12.0 %all-to-all-done.atom_ref.refs_0_.refs_1_.vec_ref = f32[16,64,128]{2,1,0:T(8,128)S(1)} async-done(((f32[16,64,128]{2,1,0:T(8,128)}), f32[16,64,128]{2,1,0:T(8,128)S(1)}, u32[]{:S(2)}, u32[]{:S(2)}) %all-to-all-start) | async-done | bytes 524320 | tf_op jit(solution)/shard_map/all_to_all | solution.py:729
  32.4 16.0 %prep.1 = (bf16[128,256,256]{2,1,0:T(8,128)(2,1)}, f32[128,16,128]{2,1,0:T(8,128)}) custom-call(f32[16,64,128]{2,1,0:T(8,128)} %copy-done, f32[128,128]{1,0:T(8,128)} %constant.38.clone.rows_ref.refs_4_, f32[10,8,128]{2,1,0:T(8,128)} %broadcast_in_dim.28.turn_ref), custom_call_target="tpu_custom_call" | custom-call | flops 2147483648 | bytes 4194304 | tf_op jit(solution)/shard_map/prep/pallas_call | solution.py:394
  48.4 16.9 %field.3 = f32[16,24,128]{2,1,0:T(8,128)} custom-call(f32[16,64,128]{2,1,0:T(8,128)} %copy-done, f32[16,64,128]{2,1,0:T(8,128)} %copy-done, bf16[128,256,256]{2,1,0:T(8,128)(2,1)} %get-tuple-element.12.refs_2_, f32[128,16,128]{2,1,0:T(8,128)} %get-tuple-element.13.refs_3_, f32[128,128]{1,0:T(8,128)} %constant.38.clone.rows_ref.refs_4_, ...), custom_call_target="tpu_custom_call" | custom-call | flops 2147483648 | bytes 4194304 | tf_op jit(solution)/shard_map/field/pallas_call | solution.py:537
  65.3 4.2 %all-to-all-start.1 = ((f32[16,24,128]{2,1,0:T(8,128)}), f32[16,24,128]{2,1,0:T(8,128)S(1)}, u32[]{:S(2)}, u32[]{:S(2)}) async-start(f32[16,24,128]{2,1,0:T(8,128)} %field.3), calls=%async_computation.1 | async-start | bytes 393216 | tf_op jit(solution)/shard_map/all_to_all | solution.py:729
  69.8 0.8 pad_bitcast_fusion.col_ref
  72.1 7.7 %pair.3.pair_ref = f32[24,128]{1,0:T(8,128)} custom-call(f32[56]{0:T(128)} %reshape.171.wts_ref, s32[1]{0:T(128)} %bitcast.4.rank_ref, f32[3,384]{1,0:T(4,128)} %copy-done.6, f32[3,1024]{1,0:T(4,128)} %pos_ref.5, f32[3,384]{1,0:T(4,128)} %copy-done.5, f32[1024,8]{1,0:T(8,128)} %pad_bitcast_fusion.col_ref, f32[16,64,128]{2,1,0:T(8,128)} %copy-done), custom_call_target="tpu_custom_call" | custom-call | flops 1073741824 | bytes 4194304 | tf_op jit(solution)/shard_map/pair/pallas_call | solution.py:608
  80.4 1.7 update.2
  82.1 15.1 %all_to_all.30.refs_0_.vec_ref = f32[16,24,128]{2,1,0:T(8,128)} all-to-all(f32[16,24,128]{2,1,0:T(8,128)} %get-tuple-element.15), channel_id=1, replica_groups=mesh['rep'=2,'gx'=16] {'gx'}, dimensions={0} | all-to-all | bytes 393216 | tf_op jit(solution)/shard_map/all_to_all | solution.py:729
  97.2 16.8 %field.4 = f32[16,24,128]{2,1,0:T(8,128)} custom-call(f32[16,24,128]{2,1,0:T(8,128)} %all_to_all.30.refs_0_.vec_ref, f32[16,64,128]{2,1,0:T(8,128)} %copy-done, bf16[128,256,256]{2,1,0:T(8,128)(2,1)} %get-tuple-element.12.refs_2_, f32[128,16,128]{2,1,0:T(8,128)} %get-tuple-element.13.refs_3_, f32[128,128]{1,0:T(8,128)} %constant.38.clone.rows_ref.refs_4_, ...), custom_call_target="tpu_custom_call" | custom-call | flops 2147483648 | bytes 4194304 | tf_op jit(solution)/shard_map/field/pallas_call | solution.py:537
  114.0 3.5 %all-to-all-start.3 = ((f32[16,24,128]{2,1,0:T(8,128)}), f32[16,24,128]{2,1,0:T(8,128)S(1)}, u32[]{:S(2)}, u32[]{:S(2)}) async-start(f32[16,24,128]{2,1,0:T(8,128)} %field.4), calls=%async_computation.3 | async-start | bytes 393216 | tf_op jit(solution)/shard_map/all_to_all | solution.py:729
  117.6 7.6 %pair.4.pair_ref = f32[24,128]{1,0:T(8,128)} custom-call(f32[56]{0:T(128)} %reshape.171.wts_ref, s32[1]{0:T(128)} %bitcast.4.rank_ref, f32[3,384]{1,0:T(4,128)} %copy-done.6, f32[3,1024]{1,0:T(4,128)} %pos_ref.5, f32[3,384]{1,0:T(4,128)} %copy-done.5, f32[1024,8]{1,0:T(8,128)} %pad_bitcast_fusion.col_ref, f32[16,24,128]{2,1,0:T(8,128)} %all_to_all.30.refs_0_.vec_ref), custom_call_target="tpu_custom_call" | custom-call | flops 1073741824 | bytes 4194304 | tf_op jit(solution)/shard_map/pair/pallas_call | solution.py:608
  125.1 1.4 all-to-all-done.3.ret_ref
  127.2 1.7 update.3
  128.9 13.7 %all_to_all.31.vec_ref.refs_0_ = f32[16,24,128]{2,1,0:T(8,128)} all-to-all(f32[16,24,128]{2,1,0:T(8,128)} %get-tuple-element.16), channel_id=1, replica_groups=mesh['rep'=2,'gx'=16] {'gx'}, dimensions={0} | all-to-all | bytes 393216 | tf_op jit(solution)/shard_map/all_to_all | solution.py:729
  142.6 7.6 %pair.5.pair_ref = f32[24,128]{1,0:T(8,128)} custom-call(f32[56]{0:T(128)} %reshape.171.wts_ref, s32[1]{0:T(128)} %bitcast.4.rank_ref, f32[3,384]{1,0:T(4,128)} %copy-done.6, f32[3,1024]{1,0:T(4,128)} %pos_ref.5, f32[3,384]{1,0:T(4,128)} %copy-done.5, f32[1024,8]{1,0:T(8,128)} %pad_bitcast_fusion.col_ref, f32[16,24,128]{2,1,0:T(8,128)} %all_to_all.31.vec_ref.refs_0_), custom_call_target="tpu_custom_call" | custom-call | flops 1073741824 | bytes 4194304 | tf_op jit(solution)/shard_map/pair/pallas_call | solution.py:608
  150.1 1.5 moments.1.refs_7_
  151.6 16.9 %field.5 = f32[16,32,128]{2,1,0:T(8,128)} custom-call(f32[16,24,128]{2,1,0:T(8,128)} %all_to_all.31.vec_ref.refs_0_, f32[16,64,128]{2,1,0:T(8,128)} %copy-done, bf16[128,256,256]{2,1,0:T(8,128)(2,1)} %get-tuple-element.12.refs_2_, f32[128,16,128]{2,1,0:T(8,128)} %get-tuple-element.13.refs_3_, f32[128,128]{1,0:T(8,128)} %constant.38.clone.rows_ref.refs_4_, ...), custom_call_target="tpu_custom_call" | custom-call | flops 2147483648 | bytes 4194304 | tf_op jit(solution)/shard_map/field/pallas_call | solution.py:537
  168.5 14.2 %all_to_all.32.ret_ref = f32[16,32,128]{2,1,0:T(8,128)} all-to-all(f32[16,32,128]{2,1,0:T(8,128)} %field.5), channel_id=1, replica_groups=mesh['rep'=2,'gx'=16] {'gx'}, dimensions={0} | all-to-all | bytes 524288 | tf_op jit(solution)/shard_map/all_to_all | solution.py:729
  182.7 1.7 finish.1
  (40 shorter events, 6.5 us)
Async XLA Ops:
  0.6 68.9 %copy-start.3 = (f32[3,1024]{1,0:T(4,128)S(1)}, f32[3,1024]{1,0:T(4,128)}, u32[]{:S(2)}) copy-start(f32[3,1024]{1,0:T(4,128)} %pos_ref.5) | copy-start | bytes 36868
  1.4 70.1 %collective-permute-start.1 = (f32[3,384]{1,0:T(4,128)S(1)}, f32[3,384]{1,0:T(4,128)S(1)}, u32[]{:S(2)}, u32[]{:S(2)}) collective-permute-start(f32[3,384]{1,0:T(4,128)S(1)} %get-tuple-element.20), channel_id=1, source_target_pairs={{1,0},{2,1},{3,2},{4,3},{5,4},{6,5},{7,6},{8,7},{9,8},{10,9},{11,1... | collective-permute-start | bytes 13832 | tf_op jit(solution)/shard_map/ppermute | solution.py:746
  6.8 64.6 %collective-permute-start = (f32[3,384]{1,0:T(4,128)S(1)}, f32[3,384]{1,0:T(4,128)S(1)}, u32[]{:S(2)}, u32[]{:S(2)}) collective-permute-start(f32[3,384]{1,0:T(4,128)S(1)} %get-tuple-element.21), channel_id=1, source_target_pairs={{0,1},{1,2},{2,3},{3,4},{4,5},{5,6},{6,7},{7,8},{8,9},{9,10},{10,1... | collective-permute-start | bytes 13832 | tf_op jit(solution)/shard_map/ppermute | solution.py:745
  8.3 61.5 %copy-start.4 = (s32[8,7]{1,0:T(8,128)S(1)}, s32[8,7]{1,0:T(8,128)}, u32[]{:S(2)}) copy-start(s32[8,7]{1,0:T(8,128)} %param.14) | copy-start | bytes 676
  11.5 20.1 %all-to-all-start = ((f32[16,64,128]{2,1,0:T(8,128)}), f32[16,64,128]{2,1,0:T(8,128)S(1)}, u32[]{:S(2)}, u32[]{:S(2)}) async-start(f32[16,64,128]{2,1,0:T(8,128)} %get-tuple-element.11), calls=%async_computation | async-start | bytes 1048576 | tf_op jit(solution)/shard_map/all_to_all | solution.py:729
  31.6 0.8 copy-start
  65.3 14.4 %all-to-all-start.1 = ((f32[16,24,128]{2,1,0:T(8,128)}), f32[16,24,128]{2,1,0:T(8,128)S(1)}, u32[]{:S(2)}, u32[]{:S(2)}) async-start(f32[16,24,128]{2,1,0:T(8,128)} %field.3), calls=%async_computation.1 | async-start | bytes 393216 | tf_op jit(solution)/shard_map/all_to_all | solution.py:729
  71.5 0.6 copy-start.5
  71.5 0.6 copy-start.6
  79.7 0.7 copy-start.1
  114.0 12.5 %all-to-all-start.3 = ((f32[16,24,128]{2,1,0:T(8,128)}), f32[16,24,128]{2,1,0:T(8,128)S(1)}, u32[]{:S(2)}, u32[]{:S(2)}) async-start(f32[16,24,128]{2,1,0:T(8,128)} %field.4), calls=%async_computation.3 | async-start | bytes 393216 | tf_op jit(solution)/shard_map/all_to_all | solution.py:729
  126.5 0.7 copy-start.2
where the time goes:
time: 186 us; the launch traced here: 184 us
  Pallas kernels  99.2 us (53%)
  blocking collectives  43 us (23%)
  starting transfers between devices  19 us (10%)
  waiting for transfers between devices  13.3 us (7%)
  local copies, waits for them, and re-layouts  7.09 us (4%)
  other arithmetic  2.06 us (1%)
    pallas_call x3, Pallas kernels, field_call(): pl.pallas_call(lambda *refs: field_kernel(sums is not None, *refs), in_sp...  50.7 us
    all_to_all x3, blocking collectives, swap(): return lax.all_to_all(x, 'gx', split_axis=0, concat_axis=0, tiled=True)  43 us
    pallas_call x3, Pallas kernels, pair_call(): pl.pallas_call(pair_kernel, in_specs=[IN_SMEM, IN_SMEM] + [IN_VMEM] * 5,...  22.8 us
    pallas_call x1, Pallas kernels, prep_call(): pl.pallas_call(prep_kernel, grid=(parts,), in_specs=[pl.BlockSpec((1, 8 *...  16 us
    all_to_all x3, starting transfers between devices, swap(): return lax.all_to_all(x, 'gx', split_axis=0, concat_axis=0, tiled=True)  13.5 us
    all_to_all x3, waiting for transfers between devices, swap(): return lax.all_to_all(x, 'gx', split_axis=0, concat_axis=0, tiled=True)  13.3 us
    ppermute x1, starting transfers between devices, per_device_modes(): right = lax.ppermute(positions[:, :halo], 'gx', down)  5.44 us
  transfers between devices with their start and end apart: 5, of which 2 were waited for; matrix products, arithmetic and copies ran while one was open for 3% of the time, Pallas kernels for 28%

commit v1 on v0

--- a/solution.py
+++ b/solution.py
@@ -63,7 +63,7 @@
         return (carried, PAIR_C * field_sum)
 
     block_ids = jnp.arange(slab_blocks, dtype=jnp.int32)
-    unused_carry, blocks_out = lax.scan(
+    _, blocks_out = lax.scan(
         one_block, jnp.zeros((), jnp.float32), (home_blocks, tile_rows, live_counts, block_ids)
     )
     return blocks_out.transpose(1, 0, 2).reshape(3, slab_blocks * TILE)
@@ -243,11 +243,12 @@
 F32 = jnp.float32
 BF16 = jnp.bfloat16
 ROWS = 8
-SPAN = 2 * HALO_BLK + 1
+LINES = 2 * ROWS
 IN_VMEM = pl.BlockSpec(memory_space=pltpu.VMEM)
 IN_SMEM = pl.BlockSpec(memory_space=pltpu.SMEM)
 IN_HBM = pl.BlockSpec(memory_space=pl.ANY)
 REACH = ORDER - 1
+PACKED = 6
 NT = (((1,), (1,)), ((), ()))
 
 
@@ -307,10 +308,10 @@
     tiles = [block_rows(field_ref, c) / inv for c in range(3)]
     for c in range(3):
         own_ref[c * blocks : (c + 1) * blocks, :] = tiles[c]
-    tiles.append(sum(float(k) * block_rows(xs_ref, k) for k in range(1, ORDER)) - 1.5)
+    tiles.append(sum(float(k) * block_rows(xs_ref.at[k], 0) for k in range(1, ORDER)) - 1.5)
     line = lax.broadcasted_iota(jnp.int32, (grid, TILE), 0)
     for axis in range(2):
-        starts, offsets = [], []
+        spots = []
         for b in range(blocks):
             here = slice(b * TILE, (b + 1) * TILE)
             value = yz_ref[2 * axis, here, :].T
@@ -319,10 +320,9 @@
             first = used * (1.0 - pltpu.roll(used, 1, 0))
             start = jnp.sum(first * line.astype(F32), axis=0, keepdims=True)
             offset = (line - start.astype(jnp.int32)) & (grid - 1)
-            starts.append(start)
-            offsets.append(jnp.sum(value * offset.astype(F32), axis=0, keepdims=True) - 1.5)
-        tiles.append(jnp.concatenate(starts, axis=0))
-        tiles.append(jnp.concatenate(offsets, axis=0))
+            shift = jnp.sum(value * offset.astype(F32), axis=0, keepdims=True) - 1.5
+            spots.append((start - float(grid // 2)) + shift)
+        tiles.append(jnp.concatenate(spots, axis=0))
     for d in range(parts):
         for i, tile in enumerate(tiles):
             out_ref[d, i * blocks : (i + 1) * blocks, :] = tile
@@ -337,7 +337,7 @@
         out_shape=[
             jax.ShapeDtypeStruct((3 * blocks, TILE), F32),
             jax.ShapeDtypeStruct((blocks, TILE), F32),
-            jax.ShapeDtypeStruct((parts, 8 * blocks, TILE), F32),
+            jax.ShapeDtypeStruct((parts, PACKED * blocks, TILE), F32),
         ],
         name="pack",
         **params(1 << 26),
@@ -345,129 +345,171 @@
 
 
 def prep_kernel(atom_ref, rows_ref, turn_ref, tab_ref, yt_ref):
-    blocks = tab_ref.shape[0]
-    grid = rows_ref.shape[0]
-    tile = lambda i: atom_ref[0, i * blocks : (i + 1) * blocks, :]
+    slabs = atom_ref.shape[0]
+    blocks = tab_ref.shape[0] // slabs
+    kept, grid = rows_ref.shape
     high, low = halves(rows_ref[...])
     twice = jnp.concatenate([high, low], axis=0).astype(BF16)
     matrix = jnp.concatenate([twice, twice], axis=1)
-    line = lax.broadcasted_iota(jnp.int32, (grid, TILE), 0)
-    start_z, u_z = tile(6).astype(jnp.int32), tile(7)
-    values, slopes = spline_values(u_z), spline_slopes(u_z)
-    spots = [(start_z + k) & (grid - 1) for k in range(ORDER)]
-    for b in range(blocks):
-        row = slice(b, b + 1)
-        dense = jnp.zeros((grid, TILE), F32)
-        tilted = dense
-        for k in range(ORDER):
-            here = line == spots[k][row]
-            dense = jnp.where(here, values[k][row], dense)
-            tilted = jnp.where(here, slopes[k][row], tilted)
-        high, low = halves(jnp.concatenate([dense, tilted], axis=1))
-        both = bdot(matrix, jnp.concatenate([high, low], axis=0).astype(BF16))
-        high, low = halves(both[:grid] + both[grid:])
-        tab_ref[b] = jnp.concatenate([high, low], axis=0).astype(BF16)
-    start_y, u_y = tile(4), tile(5)
-    values, slopes = spline_values(u_y), spline_slopes(u_y)
-    mode, sine = turn_ref[0], turn_ref[1]
+    packed = (LINES, TILE)
+    line = lax.broadcasted_iota(jnp.int32, (grid, TILE), 0).astype(F32).astype(BF16)
+    lines = [line[c * LINES : (c + 1) * LINES] for c in range(grid // LINES)]
+    turn = [jnp.broadcast_to(turn_ref[:, c : c + 1], packed) for c in range(2 * ORDER)]
     half = float(grid // 2)
-    for b in range(blocks):
-        row = slice(b, b + 1)
-        phase = (mode * start_y[row]).astype(jnp.int32) + grid // 2
-        angle = ((phase & (grid - 1)).astype(F32) - half) * (jnp.pi / (4.0 * half))
-        sq = angle * angle
-        s = angle * (1.0 + sq * (-1.0 / 6 + sq * (1.0 / 120 + sq * (-1.0 / 5040 + sq / 362880))))
-        c = 1.0 + sq * (-0.5 + sq * (1.0 / 24 + sq * (-1.0 / 720 + sq / 40320)))
-        for _ in range(2):
-            s, c = 2.0 * s * c, 1.0 - 2.0 * s * s
-        lead = jnp.where(sine > 0.0, s, c)
-        side = jnp.where(sine > 0.0, -c, s)
-        for i, weights in enumerate((values, slopes)):
-            even = weights[0][row] + sum(weights[k][row] * turn_ref[1 + k] for k in range(1, ORDER))
-            odd = sum(weights[k][row] * turn_ref[ORDER + k] for k in range(1, ORDER))
-            yt_ref[b, i * ROWS : (i + 1) * ROWS, :] = lead * even - side * odd
+
+    def spread_row(x, b):
+        return jnp.broadcast_to(x[b : b + 1], packed).astype(BF16)
+
+    def one_slab(slab, carry):
+        def located(i):
+            place = atom_ref[slab, i * blocks : (i + 1) * blocks, :]
+            start = jnp.floor(place)
+            u = place - start
+            return start, spline_values(u), spline_slopes(u)
+
+        start, values, slopes = located(5)
+        start = start.astype(jnp.int32) + grid // 2
+        spots = [((start + k) & (grid - 1)).astype(F32) for k in range(ORDER)]
+        pieces = [halves(x) for x in values], [halves(x) for x in slopes]
+        for b in range(blocks):
+            at = [spread_row(x, b) for x in spots]
+            tables = []
+            for part in range(2):
+                columns = []
+                for kind in range(2):
+                    rows = [spread_row(x[part], b) for x in pieces[kind]]
+                    column = []
+                    for here in lines:
+                        dense = jnp.zeros(packed, BF16)
+                        for k in range(ORDER):
+                            dense = jnp.where(here == at[k], rows[k], dense)
+                        column.append(dense)
+                    columns.append(jnp.concatenate(column, axis=0))
+                tables.append(jnp.concatenate(columns, axis=1))
+            both = bdot(matrix, jnp.concatenate(tables, axis=0))
+            high, low = halves(both[:kept] + both[kept:])
+            tab_ref[slab * blocks + b] = jnp.concatenate([high, low], axis=0).astype(BF16)
+        start, values, slopes = located(4)
+        mode, sine = turn[0], turn[1]
+        for b in range(blocks):
+            row = slice(b, b + 1)
+            phase = mode * start[row]
+            phase = phase - 2.0 * half * jnp.floor(phase * (0.5 / half) + 0.5)
+            angle = phase * (jnp.pi / (4.0 * half))
+            sq = angle * angle
+            s = angle * (1.0 + sq * (-1.0 / 6 + sq * (1.0 / 120 + sq * (-1.0 / 5040 + sq / 362880))))
+            c = 1.0 + sq * (-0.5 + sq * (1.0 / 24 + sq * (-1.0 / 720 + sq / 40320)))
+            for _ in range(2):
+                s, c = 2.0 * s * c, 1.0 - 2.0 * s * s
+            lead = jnp.where(sine > 0.0, s, c)
+            side = jnp.where(sine > 0.0, -c, s)
+            for i, weights in enumerate((values, slopes)):
+                even = weights[0][row] + sum(weights[k][row] * turn[1 + k] for k in range(1, ORDER))
+                odd = sum(weights[k][row] * turn[ORDER + k] for k in range(1, ORDER))
+                yt_ref[slab * blocks + b, i * LINES : (i + 1) * LINES, :] = lead * even - side * odd
+        return carry
+
+    lax.fori_loop(0, slabs, one_slab, 0)
 
 
 def prep_call(atoms, rows, turns, blocks):
     parts = atoms.shape[0]
-    grid = rows.shape[0]
+    kept = rows.shape[0]
+    slabs = 1
     return pl.pallas_call(
         prep_kernel,
-        grid=(parts,),
+        grid=(parts // slabs,),
         in_specs=[
-            pl.BlockSpec((1, 8 * blocks, TILE), lambda s: (s, 0, 0)),
+            pl.BlockSpec((slabs, PACKED * blocks, TILE), lambda s: (s, 0, 0)),
             pl.BlockSpec(rows.shape, lambda s: (0, 0)),
-            pl.BlockSpec(turns.shape, lambda s: (0, 0, 0)),
+            pl.BlockSpec(turns.shape, lambda s: (0, 0)),
         ],
         out_specs=[
-            pl.BlockSpec((blocks, 2 * grid, 2 * TILE), lambda s: (s, 0, 0)),
-            pl.BlockSpec((blocks, 2 * ROWS, TILE), lambda s: (s, 0, 0)),
+            pl.BlockSpec((slabs * blocks, 2 * kept, 2 * TILE), lambda s: (s, 0, 0)),
+            pl.BlockSpec((slabs * blocks, 2 * LINES, TILE), lambda s: (s, 0, 0)),
         ],
         out_shape=[
-            jax.ShapeDtypeStruct((parts * blocks, 2 * grid, 2 * TILE), BF16),
-            jax.ShapeDtypeStruct((parts * blocks, 2 * ROWS, TILE), F32),
+            jax.ShapeDtypeStruct((parts * blocks, 2 * kept, 2 * TILE), BF16),
+            jax.ShapeDtypeStruct((parts * blocks, 2 * LINES, TILE), F32),
         ],
         name="prep",
         **params(1 << 31),
     )(atoms, rows, turns)
 
 
-def field_kernel(with_sums, v_ref, atom_ref, tab_hbm, yt_ref, rows_ref, cols_ref, kern_ref, *rest):
+def moment_rows(energy, v0_ref, v1_ref, v2_ref, inv_ref, pair_ref):
+    ip = jnp.concatenate([inv_ref[...]] * 3, axis=0)
+    v0, v1, v2 = v0_ref[...], v1_ref[...], v2_ref[...]
+    d1, d2 = ip * v1, ip * v2
+    terms = [v0 * (ip * v0), v0 * d1, v1 * d1, v1 * d2, v2 * d2, -(v2 * pair_ref[...])]
+    rows = [jnp.sum(term, axis=0, keepdims=True) for term in terms]
+    rows[5] = rows[5] + energy
+    blank = jnp.zeros((ROWS - len(rows), TILE), F32)
+    return jnp.concatenate(rows + [blank], axis=0)
+
+
+def field_kernel(with_sums, v_ref, atom_ref, tab_hbm, yt_hbm, rows_ref, cols_ref, kern_hbm, *rest):
     if with_sums:
-        sums_ref, out_ref, tab, sem, grid_ref = rest
+        *known, out_ref, tab, sem, yt_ref, yt_sem, kern_ref, kern_sem, grid_ref = rest
     else:
-        out_ref, tab, sem, grid_ref = rest
+        out_ref, tab, sem, yt_ref, yt_sem, kern_ref, kern_sem, grid_ref = rest
     parts = out_ref.shape[0]
     grid = rows_ref.shape[0]
     blocks = tab.shape[0] // parts
-    width = ROWS * ORDER
+    width = LINES * ORDER
+    kept = grid // 2
 
     def fetch(s):
         part = pl.ds(s * blocks, blocks)
-        return pltpu.make_async_copy(tab_hbm.at[part], tab.at[part], sem.at[s])
-
+        return (
+            pltpu.make_async_copy(yt_hbm.at[part], yt_ref.at[part], yt_sem.at[s]),
+            pltpu.make_async_copy(tab_hbm.at[part], tab.at[part], sem.at[s]),
+        )
+
+    kern_copy = pltpu.make_async_copy(kern_hbm, kern_ref, kern_sem)
     for s in range(parts):
-        fetch(s).start()
+        for copy in fetch(s):
+            copy.start()
+    kern_copy.start()
     grid_ref[...] = jnp.zeros(grid_ref.shape, F32)
 
     def plane(q):
-        return pl.ds(pl.multiple_of(q * ROWS, ROWS), ROWS)
+        return pl.ds(pl.multiple_of(q * LINES, LINES), LINES)
 
     def x_weights(s):
         u = atom_ref[s, 3 * blocks : 4 * blocks, :]
         return spline_values(u), spline_slopes(u)
 
     def spread(s, carry):
-        fetch(s).wait()
+        for copy in fetch(s):
+            copy.wait()
         value, slope = x_weights(s)
         vec = [v_ref[s, c * blocks : (c + 1) * blocks, :] for c in range(3)]
         a0 = [vec[0] * slope[k] for k in range(ORDER)]
         a1 = [vec[1] * value[k] for k in range(ORDER)]
         a2 = [vec[2] * value[k] for k in range(ORDER)]
-        sums = [jnp.zeros((ROWS, grid), F32) for _ in range(blocks + REACH)]
+        sums = [jnp.zeros((LINES, grid), F32) for _ in range(blocks + REACH)]
         for b in range(blocks):
             g = s * blocks + b
             row = slice(b, b + 1)
-            yt, dyt = yt_ref[g, 0:ROWS, :], yt_ref[g, ROWS : 2 * ROWS, :]
+            yt, dyt = yt_ref[g, 0:LINES, :], yt_ref[g, LINES : 2 * LINES, :]
             lead = jnp.concatenate([a0[k][row] * yt + a1[k][row] * dyt for k in range(ORDER)], axis=0)
             tail = jnp.concatenate([a2[k][row] * yt for k in range(ORDER)], axis=0)
             high, low = halves(jnp.concatenate([lead, tail], axis=1))
             lhs = jnp.concatenate([high, low], axis=0).astype(BF16)
             out = lax.dot_general(lhs, tab[g], NT, preferred_element_type=F32)
             out = out[:width] + out[width:]
-            out = out[:, :grid] + out[:, grid:]
             for k in range(ORDER):
-                sums[b + k] = sums[b + k] + out[k * ROWS : (k + 1) * ROWS]
+                sums[b + k] = sums[b + k] + out[k * LINES : (k + 1) * LINES]
         for j, tile in enumerate(sums):
             grid_ref[plane(s * blocks + j), :] += tile
         return carry
 
     lax.fori_loop(0, parts, spread, 0)
     side = REACH // 2
-    body = slice(side * ROWS, (side + grid) * ROWS)
-    left, right = slice(0, side * ROWS), slice((side + grid) * ROWS, (2 * side + grid) * ROWS)
-    first = slice(side * ROWS, 2 * side * ROWS)
-    last = slice(grid * ROWS, (side + grid) * ROWS)
+    left, right = slice(0, side * LINES), slice((side + grid) * LINES, (2 * side + grid) * LINES)
+    first = slice(side * LINES, 2 * side * LINES)
+    last = slice(grid * LINES, (side + grid) * LINES)
     grid_ref[last, :] += grid_ref[left, :]
     grid_ref[first, :] += grid_ref[right, :]
 
@@ -481,20 +523,32 @@
         )
 
     def lines(j):
-        return pl.ds(side * ROWS + j, grid, stride=ROWS)
-
-    charge = jnp.concatenate([grid_ref[lines(j), :] for j in range(ROWS)], axis=1)
+        return pl.ds(side * LINES + j, grid, stride=LINES)
+
+    lower = lax.broadcasted_iota(jnp.int32, (grid, grid), 1) < kept
+
+    def folded(j):
+        x = grid_ref[lines(j), :]
+        return x + pltpu.roll(x, kept, 1)
+
+    charge = jnp.concatenate(
+        [jnp.where(lower, folded(j), folded(j + ROWS)) for j in range(ROWS)], axis=1
+    )
     spectrum = product(rows_ref[...], charge)
+    kern_copy.wait()
     weighted = spectrum * kern_ref[...]
     potential = product(cols_ref[...], weighted)
     for j in range(ROWS):
-        grid_ref[lines(j), :] = potential[:, j * grid : (j + 1) * grid]
+        x = potential[:, j * grid : (j + 1) * grid]
+        y = pltpu.roll(x, kept, 1)
+        grid_ref[lines(j), :] = jnp.where(lower, x, y)
+        grid_ref[lines(j + ROWS), :] = jnp.where(lower, y, x)
     grid_ref[left, :] = grid_ref[last, :]
     grid_ref[right, :] = grid_ref[first, :]
     if with_sums:
-        energy = jnp.sum(spectrum * weighted)
-        row = lax.broadcasted_iota(jnp.int32, sums_ref.shape, 0)
-        sums = sums_ref[...] + jnp.where(row == 5, energy, 0.0)
+        energy = jnp.sum(spectrum * weighted, axis=0, keepdims=True)
+        energy = sum(energy[:, j * grid : (j + 1) * grid] for j in range(ROWS))
+        sums = moment_rows(energy, *known)
         for d in range(parts):
             out_ref[d, 3 * blocks :, :] = sums
 
@@ -505,12 +559,16 @@
         for b in range(blocks):
             g = s * blocks + b
             row = slice(b, b + 1)
-            yt, dyt = yt_ref[g, 0:ROWS, :], yt_ref[g, ROWS : 2 * ROWS, :]
+            yt, dyt = yt_ref[g, 0:LINES, :], yt_ref[g, LINES : 2 * LINES, :]
             near = pieces[b : b + ORDER]
-            lhs = jnp.concatenate([x[0] for x in near] + [x[1] for x in near], axis=0).astype(BF16)
-            out = bdot(jnp.concatenate([lhs, lhs], axis=1), tab[g])
-            out = out[:width] + out[width:]
-            tiles = [out[k * ROWS : (k + 1) * ROWS] for k in range(ORDER)]
+            high = jnp.concatenate([x[0] for x in near], axis=0).astype(BF16)
+            low = jnp.concatenate([x[1] for x in near], axis=0).astype(BF16)
+            table = tab[g]
+            out = bdot(
+                jnp.concatenate([high, low], axis=1),
+                jnp.concatenate([table, table[:kept], jnp.zeros_like(table[:kept])], axis=0),
+            )
+            tiles = [out[k * LINES : (k + 1) * LINES] for k in range(ORDER)]
             f0 = sum(slope[k][row] * tiles[k][:, :TILE] for k in range(ORDER))
             f1 = sum(value[k][row] * tiles[k][:, :TILE] for k in range(ORDER))
             f2 = sum(value[k][row] * tiles[k][:, TILE:] for k in range(ORDER))
@@ -523,37 +581,41 @@
     lax.fori_loop(0, parts, gather, 0)
 
 
-def field_call(vec, atoms, table, yt, rows, cols, kern, sums=None):
+def field_call(vec, atoms, table, yt, rows, cols, kern, known=()):
     parts = vec.shape[0]
     grid = rows.shape[0]
     blocks = yt.shape[0] // parts
     args = [vec, atoms, table, yt, rows, cols, kern]
-    specs = [IN_VMEM, IN_VMEM, IN_HBM] + [IN_VMEM] * 4
+    specs = [IN_VMEM, IN_VMEM, IN_HBM, IN_HBM, IN_VMEM, IN_VMEM, IN_HBM]
     out_rows = 3 * blocks
-    if sums is not None:
-        args.append(sums)
-        specs.append(IN_VMEM)
+    if known:
+        args.extend(known)
+        specs.extend([IN_VMEM] * len(known))
         out_rows += ROWS
     return pl.pallas_call(
-        lambda *refs: field_kernel(sums is not None, *refs),
+        lambda *refs: field_kernel(len(known) > 0, *refs),
         in_specs=specs,
         out_specs=IN_VMEM,
         out_shape=jax.ShapeDtypeStruct((parts, out_rows, TILE), F32),
         scratch_shapes=[
             pltpu.VMEM(table.shape, BF16),
             pltpu.SemaphoreType.DMA((parts,)),
-            pltpu.VMEM(((grid + REACH) * ROWS, grid), F32),
+            pltpu.VMEM(yt.shape, F32),
+            pltpu.SemaphoreType.DMA((parts,)),
+            pltpu.VMEM(kern.shape, F32),
+            pltpu.SemaphoreType.DMA(()),
+            pltpu.VMEM(((grid + REACH) * LINES, grid), F32),
         ],
         name="field",
         **params(1 << 31, 56 << 20),
     )(*args)
 
 
-def pair_kernel(wts_ref, rank_ref, left_ref, pos_ref, right_ref, col_ref, vec_ref, out_ref, acc_ref, near_ref):
+def pair_kernel(list_ref, count_ref, rank_ref, left_ref, pos_ref, right_ref, col_ref, vec_ref, out_ref, acc_ref, near_ref):
     blocks = pos_ref.shape[1] // TILE
     ext = blocks + 2 * HALO_BLK
     total = vec_ref.shape[0] * blocks
-    chunk = 32
+    chunk = TILE // 2
     shift = 1.0 * blocks
     for c in range(3):
         for j in range(ext):
@@ -570,32 +632,37 @@
             src = lax.div(g, blocks)
             near_ref[j, 3 + c : 4 + c, :] = vec_ref[src, pl.ds(c * blocks + g - src * blocks, 1), :]
 
+    shape = (chunk, TILE)
+    ahead = lax.broadcasted_iota(jnp.int32, shape, 1) - lax.broadcasted_iota(jnp.int32, shape, 0)
+
     def one_block(b, carry):
         for c in range(TILE // chunk):
             home = col_ref[pl.ds(pl.multiple_of(b * TILE + c * chunk, chunk), chunk), :]
-            shape = (chunk, TILE)
             hx = jnp.broadcast_to(home[:, 0:1], shape)
             hy = jnp.broadcast_to(home[:, 1:2], shape)
             hz = jnp.broadcast_to(home[:, 2:3], shape)
-            sx = sy = sz = jnp.zeros(shape, F32)
-            for e in range(SPAN):
-                near = near_ref[b + e]
+
+            def one_tile(k, sums):
+                sx, sy, sz = sums
+                j = list_ref[b, k]
+                near = near_ref[j]
                 dx, dy, dz = hx - near[0:1], hy - near[1:2], hz - near[2:3]
                 vx, vy, vz = near[3:4], near[4:5], near[5:6]
                 inverse = lax.rsqrt(dx * dx + dy * dy + dz * dz + 1.0)
                 square = inverse * inverse
-                third = wts_ref[b * SPAN + e] * (inverse * square)
-                if e == HALO_BLK:
-                    row = lax.broadcasted_iota(jnp.int32, shape, 0) + c * chunk
-                    lane = lax.broadcasted_iota(jnp.int32, shape, 1)
-                    third = jnp.where(row == lane, 0.0, third)
-                fifth = 3.0 * (third * square) * (dx * vx + dy * vy + dz * vz)
-                sx = sx + (third * vx - fifth * dx)
-                sy = sy + (third * vy - fifth * dy)
-                sz = sz + (third * vz - fifth * dz)
-            acc_ref[0, pl.ds(c * chunk, chunk), :] = sx
-            acc_ref[1, pl.ds(c * chunk, chunk), :] = sy
-            acc_ref[2, pl.ds(c * chunk, chunk), :] = sz
+                itself = ahead == c * chunk - (j - b - HALO_BLK) * TILE
+                third = jnp.where(itself, 0.0, inverse * square)
+                fifth = (third * square) * (3.0 * (dx * vx + dy * vy + dz * vz))
+                return (
+                    sx + (third * vx - fifth * dx),
+                    sy + (third * vy - fifth * dy),
+                    sz + (third * vz - fifth * dz),
+                )
+
+            zero = jnp.zeros(shape, F32)
+            sums = lax.fori_loop(0, count_ref[b], one_tile, (zero, zero, zero))
+            for i in range(3):
+                acc_ref[i, c * chunk : (c + 1) * chunk, :] = sums[i]
         for i in range(3):
             out_ref[pl.ds(i * blocks + b, 1), :] = PAIR_C * jnp.sum(acc_ref[i].T, axis=0, keepdims=True)
         return carry
@@ -603,11 +670,11 @@
     lax.fori_loop(0, blocks, one_block, 0)
 
 
-def pair_call(wts, rank, left, pos, right, cols, vec):
+def pair_call(tiles, counts, rank, left, pos, right, cols, vec):
     blocks = pos.shape[1] // TILE
     return pl.pallas_call(
         pair_kernel,
-        in_specs=[IN_SMEM, IN_SMEM] + [IN_VMEM] * 5,
+        in_specs=[IN_SMEM] * 3 + [IN_VMEM] * 5,
         out_specs=IN_VMEM,
         out_shape=jax.ShapeDtypeStruct((3 * blocks, TILE), F32),
         scratch_shapes=[
@@ -616,7 +683,7 @@
         ],
         name="pair",
         **params(1 << 30),
-    )(wts, rank, left, pos, right, cols, vec)
+    )(tiles, counts, rank, left, pos, right, cols, vec)
 
 
 def update_kernel(ret_ref, pair_ref, inv_ref, own_ref, out_ref):
@@ -644,33 +711,10 @@
     )(returned, pair, inv)
 
 
-def moments_kernel(v0_ref, v1_ref, v2_ref, inv_ref, pair_ref, out_ref):
-    ip = jnp.concatenate([inv_ref[...]] * 3, axis=0)
-    v0, v1, v2 = v0_ref[...], v1_ref[...], v2_ref[...]
-    d1, d2 = ip * v1, ip * v2
-    terms = (v0 * (ip * v0), v0 * d1, v1 * d1, v1 * d2, v2 * d2, -(v2 * pair_ref[...]))
-    row = lax.broadcasted_iota(jnp.int32, out_ref.shape, 0)
-    sums = jnp.zeros(out_ref.shape, F32)
-    for k, term in enumerate(terms):
-        sums = sums + jnp.where(row == k, jnp.sum(term), 0.0)
-    out_ref[...] = sums
-
-
-def moments_call(vectors, inv, pair):
-    return pl.pallas_call(
-        moments_kernel,
-        in_specs=[IN_VMEM] * 5,
-        out_specs=IN_VMEM,
-        out_shape=jax.ShapeDtypeStruct((ROWS, TILE), F32),
-        name="moments",
-        **params(1 << 24),
-    )(*vectors, inv, pair)
-
-
 def finish_kernel(ret_ref, pair_ref, v0_ref, v1_ref, v2_ref, inv_ref, dip_ref, res_ref):
     blocks = inv_ref.shape[0]
     summed = jnp.sum(ret_ref[...], axis=0)
-    total = summed[3 * blocks :]
+    total = jnp.sum(summed[3 * blocks :], axis=1, keepdims=True)
     h = summed[: 3 * blocks] - pair_ref[...]
     m = [total[k : k + 1, 0:1] for k in range(6)]
     s = [lax.rsqrt(m[2 * i]) for i in range(3)]
@@ -725,6 +769,13 @@
     return rows.astype(np.float32)
 
 
+def kernel_lines(x_axis, y_axis, z_axis):
+    mode_sq = x_axis[0] * x_axis[0] + y_axis[0] * y_axis[0] + z_axis[0] * z_axis[0]
+    safe_sq = jnp.where(mode_sq > 0, mode_sq, 1.0)
+    green = jnp.where(mode_sq > 0, RECIP_C * jnp.exp(-DAMP * safe_sq) / safe_sq, 0.0)
+    return green * x_axis[1] * y_axis[1] * z_axis[1]
+
+
 def swap(x):
     return lax.all_to_all(x, "gx", split_axis=0, concat_axis=0, tiled=True)
 
@@ -739,42 +790,52 @@
     down = [(j, i) for i, j in up]
 
     own, inv, packed = pack_call(
-        field, inv_polar[None, :], x_spline.reshape(2 * ORDER, atoms), yz_spline, parts
+        field, inv_polar[None, :], x_spline.transpose(1, 0, 2), yz_spline, parts
     )
     everyone = swap(packed)
-    left = lax.ppermute(positions[:, atoms - halo :], "gx", up)
-    right = lax.ppermute(positions[:, :halo], "gx", down)
+    places, everyone = lax.optimization_barrier((positions, everyone))
+    left = lax.ppermute(places[:, atoms - halo :], "gx", up)
+    right = lax.ppermute(places[:, :halo], "gx", down)
     home_cols = jnp.pad(positions, ((0, ROWS - 3), (0, 0))).T
-
-    offsets = jnp.arange(SPAN, dtype=jnp.int32)
-    block_ids = jnp.arange(blocks, dtype=jnp.int32)
-    live = jnp.arange(tile_list.shape[1], dtype=jnp.int32)[None, :] < tile_count[:, None]
-    hit = tile_list[:, :, None] == block_ids[:, None, None] + offsets[None, None, :]
-    wts = jnp.sum((hit & live[:, :, None]).astype(F32), axis=1).reshape(-1)
 
     matrix = fourier_matrix(GRID)
     rows, cols = jnp.asarray(matrix), jnp.asarray(matrix.T)
     all_freq = jnp.arange(GRID, dtype=jnp.int32)
-    ky_count = GRID // parts
-    ky_freq = rank * ky_count + jnp.arange(ky_count, dtype=jnp.int32)
+    kept = GRID // 2
+    ky_freq = rank // 2 * LINES + jnp.arange(LINES, dtype=jnp.int32)
+    kz_freq = rank % 2 * kept + jnp.arange(kept, dtype=jnp.int32)
+    z_rows = lax.dynamic_slice_in_dim(rows, rank % 2 * kept, kept, 0)
     full_modes, full_weights = mode_of(all_freq, GRID)
     ky_modes, ky_weights = mode_of(ky_freq, GRID)
-    kern = kernel_block(full_modes, full_weights, ky_modes, ky_weights, full_modes, full_weights)
-    kern = kern.reshape(GRID, ky_count * GRID)
+    kz_modes, kz_weights = mode_of(kz_freq, GRID)
+
+    def paired_lines(x):
+        x = x.reshape(1, 2, ROWS, 1)
+        x = jnp.broadcast_to(x.transpose(0, 2, 1, 3), (1, ROWS, 2, kept))
+        return x.reshape(1, ROWS * GRID)
+
+    def repeated(x):
+        return jnp.tile(x[None, :], (1, LINES))
+
+    kern = kernel_lines(
+        (full_modes[:, None], full_weights[:, None]),
+        (paired_lines(ky_modes), paired_lines(ky_weights)),
+        (repeated(kz_modes), repeated(kz_weights)),
+    )
     steps = jnp.arange(1, ORDER).astype(F32)
     angle = steps[:, None] * ky_modes[None, :] * (2.0 * jnp.pi / GRID)
     sine = (ky_freq > GRID // 2).astype(F32)
     turns = jnp.concatenate([ky_modes[None], sine[None], jnp.cos(angle), jnp.sin(angle)])
-    turns = jnp.broadcast_to(turns[:, :, None], turns.shape + (TILE,))
-
-    table, yt = prep_call(everyone, rows, turns, blocks)
+    turns = jnp.pad(turns.T, ((0, 0), (0, TILE - turns.shape[0])))
+
+    table, yt = prep_call(everyone, z_rows, turns, blocks)
     vec, vectors = everyone, [own]
     rank_id = rank[None].astype(jnp.int32)
     for step in range(ITERS):
         last = step + 1 == ITERS
-        pair = pair_call(wts, rank_id, left, positions, right, home_cols, vec)
-        sums = moments_call(vectors, inv, pair) if last else None
-        returned = swap(field_call(vec, everyone, table, yt, rows, cols, kern, sums))
+        pair = pair_call(tile_list, tile_count, rank_id, left, positions, right, home_cols, vec)
+        known = (*vectors, inv, pair) if last else ()
+        returned = swap(field_call(vec, everyone, table, yt, rows, cols, kern, known))
         if not last:
             own, packed = update_call(returned, pair, inv)
             vectors.append(own)

time: 186 us -> 173 us (0.930)
  Pallas kernels: 99.2 us -> 88.2 us
    pallas_call x8 -> x7, Pallas kernels: 90.9 us -> 80 us  [the longest x3 43.1 us: field_call(): pl.pallas_call(lambda *refs: field_kernel(len(known) > 0, *refs), in_spec...]
    ppermute x2, waiting for transfers between devices: 0.01 us -> 4.91 us  [the longest x1 4.4 us: per_device_modes(): left = lax.ppermute(places[:, atoms - halo:], 'gx', up)]
    all_to_all x3, waiting for transfers between devices: 13.3 us -> 9.81 us  [swap(): return lax.all_to_all(x, 'gx', split_axis=0, concat_axis=0, tiled=True)]
  transfers between devices with their start and end apart: 5 -> 5, of which waited for: 2 -> 4; matrix products, arithmetic and copies ran while one was open for 3% -> 3% of each run, Pallas kernels for 28% -> 9%
where the time goes in v1:
time: 173 us; the launch traced here: 171 us
  Pallas kernels  88.2 us (51%)
  blocking collectives  41.8 us (24%)
  starting transfers between devices  18.8 us (11%)
  waiting for transfers between devices  14.7 us (8%)
  local copies, waits for them, and re-layouts  5.61 us (3%)
    pallas_call x3, Pallas kernels, field_call(): pl.pallas_call(lambda *refs: field_kernel(len(known) > 0, *refs), in_spec...  43.1 us
    all_to_all x3, blocking collectives, swap(): return lax.all_to_all(x, 'gx', split_axis=0, concat_axis=0, tiled=True)  41.8 us
    pallas_call x3, Pallas kernels, pair_call(): pl.pallas_call(pair_kernel, in_specs=[IN_SMEM] * 3 + [IN_VMEM] * 5, out_s...  23.2 us
    all_to_all x3, starting transfers between devices, swap(): return lax.all_to_all(x, 'gx', split_axis=0, concat_axis=0, tiled=True)  14.5 us
    pallas_call x1, Pallas kernels, prep_call(): pl.pallas_call(prep_kernel, grid=(parts // slabs,), in_specs=[pl.BlockSpe...  13.6 us
    all_to_all x3, waiting for transfers between devices, swap(): return lax.all_to_all(x, 'gx', split_axis=0, concat_axis=0, tiled=True)  9.81 us
    ppermute x1, waiting for transfers between devices, per_device_modes(): left = lax.ppermute(places[:, atoms - halo:], 'gx', up)  4.4 us
    ppermute x1, starting transfers between devices, per_device_modes(): right = lax.ppermute(places[:, :halo], 'gx', down)  4.37 us
  transfers between devices with their start and end apart: 5, of which 4 were waited for; matrix products, arithmetic and copies ran while one was open for 3% of the time, Pallas kernels for 9%

profile of v1, /device:TPU:0, one launch (start us, length us, event | category | flops | bytes accessed | tf_op | source)
XLA Modules:
  0.0 171.3 jit_solution(5376686346835733858)
XLA Ops:
  0.7 3.1 %pack.1 = (f32[24,128]{1,0:T(8,128)}, f32[8,128]{1,0:T(8,128)}, f32[16,48,128]{2,1,0:T(8,128)}) custom-call(f32[3,1024]{1,0:T(4,128)} %field_ref.1, f32[1,1024]{1,0:T(1,128)} %bitcast.16, f32[5,2,1024]{2,1,0:T(2,128)} %bitcast.15, f32[4,1024,128]{2,1,0:T(8,128)} %yz_ref.1), custom_call_target="tpu_custom_call" | custom-call | flops 67108864 | bytes 4194304 | tf_op jit(solution)/shard_map/pack/pallas_call | solution.py:333
  3.8 7.4 %all-to-all-start = ((f32[16,48,128]{2,1,0:T(8,128)}), f32[16,48,128]{2,1,0:T(8,128)S(1)}, u32[]{:S(2)}, u32[]{:S(2)}) async-start(f32[16,48,128]{2,1,0:T(8,128)} %get-tuple-element.13), calls=%async_computation | async-start | bytes 786432 | tf_op jit(solution)/shard_map/all_to_all | solution.py:780
  13.6 1.1 fusion.2.refs_6_
  14.7 8.6 %all-to-all-done.atom_ref.refs_0_.refs_1_.vec_ref = f32[16,48,128]{2,1,0:T(8,128)S(1)} async-done(((f32[16,48,128]{2,1,0:T(8,128)}), f32[16,48,128]{2,1,0:T(8,128)S(1)}, u32[]{:S(2)}, u32[]{:S(2)}) %all-to-all-start) | async-done | bytes 393248 | tf_op jit(solution)/shard_map/all_to_all | solution.py:780
  23.3 0.8 copy-done
  24.1 13.6 %prep.1 = (bf16[128,128,256]{2,1,0:T(8,128)(2,1)}, f32[128,32,128]{2,1,0:T(8,128)}) custom-call(f32[16,48,128]{2,1,0:T(8,128)} %copy-done, f32[64,128]{1,0:T(8,128)} %constant_dynamic-slice_fusion.rows_ref, f32[16,128]{1,0:T(8,128)} %pad.8.turn_ref), custom_call_target="tpu_custom_call" | custom-call | flops 2147483648 | bytes 4194304 | tf_op jit(solution)/shard_map/prep/pallas_call | solution.py:419
  37.7 14.4 %field.3 = f32[16,24,128]{2,1,0:T(8,128)} custom-call(f32[16,48,128]{2,1,0:T(8,128)} %copy-done, f32[16,48,128]{2,1,0:T(8,128)} %copy-done, bf16[128,128,256]{2,1,0:T(8,128)(2,1)} %get-tuple-element.15.refs_2_, f32[128,32,128]{2,1,0:T(8,128)} %get-tuple-element.16.refs_3_, f32[128,128]{1,0:T(8,128)} %constant.71.clone.refs_4_, ...), custom_call_target="tpu_custom_call" | custom-call | flops 2147483648 | bytes 4194304 | tf_op jit(solution)/shard_map/field/pallas_call | solution.py:595
  52.2 3.5 %all-to-all-start.1 = ((f32[16,24,128]{2,1,0:T(8,128)}), f32[16,24,128]{2,1,0:T(8,128)S(1)}, u32[]{:S(2)}, u32[]{:S(2)}) async-start(f32[16,24,128]{2,1,0:T(8,128)} %field.3), calls=%async_computation.1 | async-start | bytes 393216 | tf_op jit(solution)/shard_map/all_to_all | solution.py:780
  55.7 4.4 %collective-permute-start.1 = (f32[3,384]{1,0:T(4,128)S(1)}, f32[3,384]{1,0:T(4,128)S(1)}, u32[]{:S(2)}, u32[]{:S(2)}) collective-permute-start(f32[3,384]{1,0:T(4,128)S(1)} %get-tuple-element.24), channel_id=1, source_target_pairs={{1,0},{2,1},{3,2},{4,3},{5,4},{6,5},{7,6},{8,7},{9,8},{10,9},{11,1... | collective-permute-start | bytes 13832 | tf_op jit(solution)/shard_map/ppermute | solution.py:798
  60.1 0.8 pad_bitcast_fusion.col_ref
  61.4 4.4 %collective-permute-done.left_ref = f32[3,384]{1,0:T(4,128)S(1)} collective-permute-done((f32[3,384]{1,0:T(4,128)S(1)}, f32[3,384]{1,0:T(4,128)S(1)}, u32[]{:S(2)}, u32[]{:S(2)}) %collective-permute-start) | collective-permute-done | bytes 4640 | tf_op jit(solution)/shard_map/ppermute | solution.py:797
  66.4 7.8 %pair.3.pair_ref = f32[24,128]{1,0:T(8,128)} custom-call(s32[8,7]{1,0:T(8,128)} %list_ref.5, s32[8]{0:T(128)} %count_ref.5, s32[1]{0:T(128)} %bitcast.7.rank_ref, f32[3,384]{1,0:T(4,128)} %copy-done.6, f32[3,1024]{1,0:T(4,128)} %pos_ref.5, f32[3,384]{1,0:T(4,128)} %copy-done.5, f32[1024,8]{1,0:T(8,128)} %pad_bitcast_fusion.col_ref, f32[16,48,128]{2,1,0:T(8,128)} %copy-done), custom_call_target="tpu_custom_call" | custom-call | flops 1073741824 | bytes 4194304 | tf_op jit(solution)/shard_map/pair/pallas_call | solution.py:675
  74.9 1.6 update.2
  76.5 13.1 %all_to_all.30.refs_0_.vec_ref = f32[16,24,128]{2,1,0:T(8,128)} all-to-all(f32[16,24,128]{2,1,0:T(8,128)} %get-tuple-element.19), channel_id=1, replica_groups=mesh['rep'=2,'gx'=16] {'gx'}, dimensions={0} | all-to-all | bytes 393216 | tf_op jit(solution)/shard_map/all_to_all | solution.py:780
  89.7 14.3 %field.4 = f32[16,24,128]{2,1,0:T(8,128)} custom-call(f32[16,24,128]{2,1,0:T(8,128)} %all_to_all.30.refs_0_.vec_ref, f32[16,48,128]{2,1,0:T(8,128)} %copy-done, bf16[128,128,256]{2,1,0:T(8,128)(2,1)} %get-tuple-element.15.refs_2_, f32[128,32,128]{2,1,0:T(8,128)} %get-tuple-element.16.refs_3_, f32[128,128]{1,0:T(8,128)} %constant.71.clone.refs_4_, ...), custom_call_target="tpu_custom_call" | custom-call | flops 2147483648 | bytes 4194304 | tf_op jit(solution)/shard_map/field/pallas_call | solution.py:595
  104.0 3.5 %all-to-all-start.3 = ((f32[16,24,128]{2,1,0:T(8,128)}), f32[16,24,128]{2,1,0:T(8,128)S(1)}, u32[]{:S(2)}, u32[]{:S(2)}) async-start(f32[16,24,128]{2,1,0:T(8,128)} %field.4), calls=%async_computation.3 | async-start | bytes 393216 | tf_op jit(solution)/shard_map/all_to_all | solution.py:780
  107.5 7.7 %pair.4.pair_ref = f32[24,128]{1,0:T(8,128)} custom-call(s32[8,7]{1,0:T(8,128)} %list_ref.5, s32[8]{0:T(128)} %count_ref.5, s32[1]{0:T(128)} %bitcast.7.rank_ref, f32[3,384]{1,0:T(4,128)} %copy-done.6, f32[3,1024]{1,0:T(4,128)} %pos_ref.5, f32[3,384]{1,0:T(4,128)} %copy-done.5, f32[1024,8]{1,0:T(8,128)} %pad_bitcast_fusion.col_ref, ...), custom_call_target="tpu_custom_call" | custom-call | flops 1073741824 | bytes 4194304 | tf_op jit(solution)/shard_map/pair/pallas_call | solution.py:675
  115.2 1.2 all-to-all-done.3.ret_ref
  117.1 1.7 update.3
  118.8 14.4 %all_to_all.31.vec_ref.refs_0_ = f32[16,24,128]{2,1,0:T(8,128)} all-to-all(f32[16,24,128]{2,1,0:T(8,128)} %get-tuple-element.20), channel_id=1, replica_groups=mesh['rep'=2,'gx'=16] {'gx'}, dimensions={0} | all-to-all | bytes 393216 | tf_op jit(solution)/shard_map/all_to_all | solution.py:780
  133.2 7.7 %pair.5.refs_11_.pair_ref = f32[24,128]{1,0:T(8,128)} custom-call(s32[8,7]{1,0:T(8,128)} %list_ref.5, s32[8]{0:T(128)} %count_ref.5, s32[1]{0:T(128)} %bitcast.7.rank_ref, f32[3,384]{1,0:T(4,128)} %copy-done.6, f32[3,1024]{1,0:T(4,128)} %pos_ref.5, f32[3,384]{1,0:T(4,128)} %copy-done.5, f32[1024,8]{1,0:T(8,128)} %pad_bitcast_fusion.col_ref, ...), custom_call_target="tpu_custom_call" | custom-call | flops 1073741824 | bytes 4194304 | tf_op jit(solution)/shard_map/pair/pallas_call | solution.py:675
  140.9 14.4 %field.5 = f32[16,32,128]{2,1,0:T(8,128)} custom-call(f32[16,24,128]{2,1,0:T(8,128)} %all_to_all.31.vec_ref.refs_0_, f32[16,48,128]{2,1,0:T(8,128)} %copy-done, bf16[128,128,256]{2,1,0:T(8,128)(2,1)} %get-tuple-element.15.refs_2_, f32[128,32,128]{2,1,0:T(8,128)} %get-tuple-element.16.refs_3_, f32[128,128]{1,0:T(8,128)} %constant.71.clone.refs_4_, ...), custom_call_target="tpu_custom_call" | custom-call | flops 2147483648 | bytes 4194304 | tf_op jit(solution)/shard_map/field/pallas_call | solution.py:595
  155.3 14.2 %all_to_all.32.ret_ref = f32[16,32,128]{2,1,0:T(8,128)} all-to-all(f32[16,32,128]{2,1,0:T(8,128)} %field.5), channel_id=1, replica_groups=mesh['rep'=2,'gx'=16] {'gx'}, dimensions={0} | all-to-all | bytes 524288 | tf_op jit(solution)/shard_map/all_to_all | solution.py:780
  169.5 1.8 %finish.1 = (f32[3,1024]{1,0:T(4,128)}, f32[3,1024]{1,0:T(4,128)}) custom-call(f32[16,32,128]{2,1,0:T(8,128)} %all_to_all.32.ret_ref, f32[24,128]{1,0:T(8,128)} %pair.5.refs_11_.pair_ref, f32[24,128]{1,0:T(8,128)} %get-tuple-element.21.refs_7_.v0_ref, f32[24,128]{1,0:T(8,128)} %get-tuple-element.22.refs_8_.v1_ref, ...), custom_call_target="tpu_custom_call" | custom-call | flops 16777216 | bytes 4194304 | tf_op jit(solution)/shard_map/finish/pallas_call | solution.py:754
  (39 shorter events, 4.8 us)
Async XLA Ops:
  0.6 12.4 %copy-start.1 = (f32[128,128]{1,0:T(8,128)S(1)}, f32[128,128]{1,0:T(8,128)}, u32[]{:S(2)}) copy-start(f32[128,128]{1,0:T(8,128)} %constant.71.clone.refs_4_) | copy-start | bytes 196612
  0.6 11.4 %copy-start.4 = (f32[3,1024]{1,0:T(4,128)S(1)}, f32[3,1024]{1,0:T(4,128)}, u32[]{:S(2)}) copy-start(f32[3,1024]{1,0:T(4,128)} %pos_ref.5) | copy-start | bytes 36868
  3.8 19.6 %all-to-all-start = ((f32[16,48,128]{2,1,0:T(8,128)}), f32[16,48,128]{2,1,0:T(8,128)S(1)}, u32[]{:S(2)}, u32[]{:S(2)}) async-start(f32[16,48,128]{2,1,0:T(8,128)} %get-tuple-element.13), calls=%async_computation | async-start | bytes 786432 | tf_op jit(solution)/shard_map/all_to_all | solution.py:780
  23.3 0.8 copy-start
  52.2 22.0 %all-to-all-start.1 = ((f32[16,24,128]{2,1,0:T(8,128)}), f32[16,24,128]{2,1,0:T(8,128)S(1)}, u32[]{:S(2)}, u32[]{:S(2)}) async-start(f32[16,24,128]{2,1,0:T(8,128)} %field.3), calls=%async_computation.1 | async-start | bytes 393216 | tf_op jit(solution)/shard_map/all_to_all | solution.py:780
  55.7 5.7 %collective-permute-start.1 = (f32[3,384]{1,0:T(4,128)S(1)}, f32[3,384]{1,0:T(4,128)S(1)}, u32[]{:S(2)}, u32[]{:S(2)}) collective-permute-start(f32[3,384]{1,0:T(4,128)S(1)} %get-tuple-element.24), channel_id=1, source_target_pairs={{1,0},{2,1},{3,2},{4,3},{5,4},{6,5},{7,6},{8,7},{9,8},{10,9},{11,1... | collective-permute-start | bytes 13832 | tf_op jit(solution)/shard_map/ppermute | solution.py:798
  60.1 5.8 %collective-permute-start = (f32[3,384]{1,0:T(4,128)S(1)}, f32[3,384]{1,0:T(4,128)S(1)}, u32[]{:S(2)}, u32[]{:S(2)}) collective-permute-start(f32[3,384]{1,0:T(4,128)S(1)} %get-tuple-element.25), channel_id=1, source_target_pairs={{0,1},{1,2},{2,3},{3,4},{4,5},{5,6},{6,7},{7,8},{8,9},{9,10},{10,1... | collective-permute-start | bytes 13832 | tf_op jit(solution)/shard_map/ppermute | solution.py:797
  61.4 4.4 %copy-start.5 = (f32[3,384]{1,0:T(4,128)}, f32[3,384]{1,0:T(4,128)S(1)}, u32[]{:S(2)}) copy-start(f32[3,384]{1,0:T(4,128)S(1)} %collective-permute-done.1.right_ref) | copy-start | bytes 13828
  65.8 0.6 copy-start.6
  74.2 0.7 copy-start.2
  104.0 12.5 %all-to-all-start.3 = ((f32[16,24,128]{2,1,0:T(8,128)}), f32[16,24,128]{2,1,0:T(8,128)S(1)}, u32[]{:S(2)}, u32[]{:S(2)}) async-start(f32[16,24,128]{2,1,0:T(8,128)} %field.4), calls=%async_computation.3 | async-start | bytes 393216 | tf_op jit(solution)/shard_map/all_to_all | solution.py:780
  116.5 0.7 copy-start.3

commit v2 on v1

--- a/solution.py
+++ b/solution.py
@@ -248,6 +248,7 @@
 IN_SMEM = pl.BlockSpec(memory_space=pltpu.SMEM)
 IN_HBM = pl.BlockSpec(memory_space=pl.ANY)
 REACH = ORDER - 1
+SPAN = 2 * HALO_BLK + 1
 PACKED = 6
 NT = (((1,), (1,)), ((), ()))
 
@@ -344,7 +345,7 @@
     )(field, inv_row, xs, yz)
 
 
-def prep_kernel(atom_ref, rows_ref, turn_ref, tab_ref, yt_ref):
+def table_maker(atom_ref, rows_ref, turn_ref, tab_ref, yt_ref):
     slabs = atom_ref.shape[0]
     blocks = tab_ref.shape[0] // slabs
     kept, grid = rows_ref.shape
@@ -360,7 +361,7 @@
     def spread_row(x, b):
         return jnp.broadcast_to(x[b : b + 1], packed).astype(BF16)
 
-    def one_slab(slab, carry):
+    def one_slab(slab):
         def located(i):
             place = atom_ref[slab, i * blocks : (i + 1) * blocks, :]
             start = jnp.floor(place)
@@ -407,34 +408,68 @@
                 even = weights[0][row] + sum(weights[k][row] * turn[1 + k] for k in range(1, ORDER))
                 odd = sum(weights[k][row] * turn[ORDER + k] for k in range(1, ORDER))
                 yt_ref[slab * blocks + b, i * LINES : (i + 1) * LINES, :] = lead * even - side * odd
-        return carry
-
-    lax.fori_loop(0, slabs, one_slab, 0)
-
-
-def prep_call(atoms, rows, turns, blocks):
-    parts = atoms.shape[0]
-    kept = rows.shape[0]
-    slabs = 1
-    return pl.pallas_call(
-        prep_kernel,
-        grid=(parts // slabs,),
-        in_specs=[
-            pl.BlockSpec((slabs, PACKED * blocks, TILE), lambda s: (s, 0, 0)),
-            pl.BlockSpec(rows.shape, lambda s: (0, 0)),
-            pl.BlockSpec(turns.shape, lambda s: (0, 0)),
-        ],
-        out_specs=[
-            pl.BlockSpec((slabs * blocks, 2 * kept, 2 * TILE), lambda s: (s, 0, 0)),
-            pl.BlockSpec((slabs * blocks, 2 * LINES, TILE), lambda s: (s, 0, 0)),
-        ],
-        out_shape=[
-            jax.ShapeDtypeStruct((parts * blocks, 2 * kept, 2 * TILE), BF16),
-            jax.ShapeDtypeStruct((parts * blocks, 2 * LINES, TILE), F32),
-        ],
-        name="prep",
-        **params(1 << 31),
-    )(atoms, rows, turns)
+
+    return one_slab
+
+
+def near_tiles(refs, vec_ref, near_ref, col_ref):
+    rank_ref, left_ref, pos_ref, right_ref = refs
+    blocks = pos_ref.shape[1] // TILE
+    total = vec_ref.shape[0] * blocks
+    shift = 1.0 * blocks
+    for j in range(blocks + 2 * HALO_BLK):
+        i = j - HALO_BLK
+        g = rank_ref[0] * blocks + i
+        if i < 0:
+            g = jnp.where(g < 0, g + total, g)
+            source, i, move = left_ref, j, -shift
+        elif i < blocks:
+            source, move = pos_ref, 0.0
+        else:
+            g = jnp.where(g >= total, g - total, g)
+            source, i, move = right_ref, i - blocks, shift
+        rows = source[:, i * TILE : (i + 1) * TILE]
+        near_ref[j, 0:1, :] = rows[0:1] + move
+        near_ref[j, 1:3, :] = rows[1:3]
+        src = lax.shift_right_logical(g, 3)
+        block = g & (ROWS - 1)
+        for c in range(3):
+            near_ref[j, 3 + c : 4 + c, :] = vec_ref[src, pl.ds(c * blocks + block, 1), :]
+        near_ref[j, 6:8, :] = jnp.zeros((2, TILE), F32)
+    for b in range(blocks):
+        col_ref[b * TILE : (b + 1) * TILE, :] = near_ref[HALO_BLK + b].T
+
+
+def pair_part(part, size, wts_ref, near_ref, col_ref, sum_ref):
+    first = part * size
+    b = lax.shift_right_logical(first, 7)
+    chunk = min(size, 32)
+    shape = (chunk, TILE)
+    lane = lax.broadcasted_iota(jnp.int32, shape, 1)
+    ahead = lane - lax.broadcasted_iota(jnp.int32, shape, 0)
+    for c in range(size // chunk):
+        start = pl.multiple_of(first + c * chunk, chunk)
+        home = col_ref[pl.ds(start, chunk), :]
+        hx = jnp.broadcast_to(home[:, 0:1], shape)
+        hy = jnp.broadcast_to(home[:, 1:2], shape)
+        hz = jnp.broadcast_to(home[:, 2:3], shape)
+        sx = sy = sz = jnp.zeros(shape, F32)
+        for e in range(SPAN):
+            near = near_ref[b + e]
+            dx, dy, dz = hx - near[0:1], hy - near[1:2], hz - near[2:3]
+            vx, vy, vz = near[3:4], near[4:5], near[5:6]
+            inverse = lax.rsqrt(dx * dx + dy * dy + dz * dz + 1.0)
+            square = inverse * inverse
+            third = wts_ref[b * SPAN + e] * (inverse * square)
+            if e == HALO_BLK:
+                third = jnp.where(ahead == start - b * TILE, 0.0, third)
+            fifth = (third * square) * (3.0 * (dx * vx + dy * vy + dz * vz))
+            sx = sx + (third * vx - fifth * dx)
+            sy = sy + (third * vy - fifth * dy)
+            sz = sz + (third * vz - fifth * dz)
+        sums = [jnp.sum(x, axis=1, keepdims=True) for x in (sx, sy, sz)]
+        both = jnp.where(lane == 0, sums[0], jnp.where(lane == 1, sums[1], sums[2]))
+        sum_ref[pl.ds(start, chunk), :] = both[:, :ROWS]
 
 
 def moment_rows(energy, v0_ref, v1_ref, v2_ref, inv_ref, pair_ref):
@@ -448,30 +483,48 @@
     return jnp.concatenate(rows + [blank], axis=0)
 
 
-def field_kernel(with_sums, v_ref, atom_ref, tab_hbm, yt_hbm, rows_ref, cols_ref, kern_hbm, *rest):
-    if with_sums:
-        *known, out_ref, tab, sem, yt_ref, yt_sem, kern_ref, kern_sem, grid_ref = rest
+def field_kernel(mode, *refs):
+    making, closing = mode
+    v_ref, rows_ref, cols_ref, kern_hbm, *refs = refs
+    if making:
+        z_ref, turn_ref, out_ref, tab_hbm, yt_hbm, *refs = refs
+        atom_ref = v_ref
+    elif closing:
+        atom_ref, tab_hbm, yt_hbm, wts_ref, *refs = refs
+        places, known, refs = refs[:4], refs[4:8], refs[8:]
+        out_ref, pair_ref, *refs = refs
     else:
-        out_ref, tab, sem, yt_ref, yt_sem, kern_ref, kern_sem, grid_ref = rest
+        atom_ref, tab_hbm, yt_hbm, out_ref, *refs = refs
+    tab, sem, yt_ref, yt_sem, kern_ref, kern_sem, grid_ref, *refs = refs
     parts = out_ref.shape[0]
     grid = rows_ref.shape[0]
     blocks = tab.shape[0] // parts
     width = LINES * ORDER
     kept = grid // 2
 
-    def fetch(s):
+    def table_copies(s):
         part = pl.ds(s * blocks, blocks)
-        return (
-            pltpu.make_async_copy(yt_hbm.at[part], yt_ref.at[part], yt_sem.at[s]),
-            pltpu.make_async_copy(tab_hbm.at[part], tab.at[part], sem.at[s]),
-        )
+        ends = [(yt_hbm.at[part], yt_ref.at[part]), (tab_hbm.at[part], tab.at[part])]
+        if making:
+            ends = [(here, there) for there, here in ends]
+        return [
+            pltpu.make_async_copy(ends[0][0], ends[0][1], yt_sem.at[s]),
+            pltpu.make_async_copy(ends[1][0], ends[1][1], sem.at[s]),
+        ]
 
     kern_copy = pltpu.make_async_copy(kern_hbm, kern_ref, kern_sem)
-    for s in range(parts):
-        for copy in fetch(s):
-            copy.start()
+    if not making:
+        for s in range(parts):
+            for copy in table_copies(s):
+                copy.start()
     kern_copy.start()
     grid_ref[...] = jnp.zeros(grid_ref.shape, F32)
+    if making:
+        make_tables = table_maker(atom_ref, z_ref, turn_ref, tab, yt_ref)
+    if closing:
+        near_ref, col_ref, sum_ref = refs
+        near_tiles(places, v_ref, near_ref, col_ref)
+        pair_size = blocks * TILE // parts
 
     def plane(q):
         return pl.ds(pl.multiple_of(q * LINES, LINES), LINES)
@@ -481,8 +534,10 @@
         return spline_values(u), spline_slopes(u)
 
     def spread(s, carry):
-        for copy in fetch(s):
-            copy.wait()
+        if making:
+            make_tables(s)
+        for copy in table_copies(s):
+            copy.start() if making else copy.wait()
         value, slope = x_weights(s)
         vec = [v_ref[s, c * blocks : (c + 1) * blocks, :] for c in range(3)]
         a0 = [vec[0] * slope[k] for k in range(ORDER)]
@@ -545,14 +600,13 @@
         grid_ref[lines(j + ROWS), :] = jnp.where(lower, y, x)
     grid_ref[left, :] = grid_ref[last, :]
     grid_ref[right, :] = grid_ref[first, :]
-    if with_sums:
+    if closing:
         energy = jnp.sum(spectrum * weighted, axis=0, keepdims=True)
         energy = sum(energy[:, j * grid : (j + 1) * grid] for j in range(ROWS))
-        sums = moment_rows(energy, *known)
-        for d in range(parts):
-            out_ref[d, 3 * blocks :, :] = sums
 
     def gather(s, carry):
+        if closing:
+            pair_part(s, pair_size, wts_ref, near_ref, col_ref, sum_ref)
         value, slope = x_weights(s)
         pieces = [halves(grid_ref[plane(s * blocks + q), :]) for q in range(blocks + REACH)]
         fields = ([], [], [])
@@ -579,59 +633,71 @@
         return carry
 
     lax.fori_loop(0, parts, gather, 0)
-
-
-def field_call(vec, atoms, table, yt, rows, cols, kern, known=()):
+    if making:
+        for s in range(parts):
+            for copy in table_copies(s):
+                copy.wait()
+    if closing:
+        for b in range(blocks):
+            turned = PAIR_C * sum_ref[b * TILE : (b + 1) * TILE, :].T
+            for c in range(3):
+                pair_ref[c * blocks + b : c * blocks + b + 1, :] = turned[c : c + 1]
+        sums = moment_rows(energy, *known, pair_ref)
+        for d in range(parts):
+            out_ref[d, 3 * blocks :, :] = sums
+
+
+def field_call(vec, rows, cols, kern, first=(), tables=(), final=()):
     parts = vec.shape[0]
     grid = rows.shape[0]
-    blocks = yt.shape[0] // parts
-    args = [vec, atoms, table, yt, rows, cols, kern]
-    specs = [IN_VMEM, IN_VMEM, IN_HBM, IN_HBM, IN_VMEM, IN_VMEM, IN_HBM]
-    out_rows = 3 * blocks
-    if known:
-        args.extend(known)
-        specs.extend([IN_VMEM] * len(known))
-        out_rows += ROWS
+    blocks = grid // parts
+    mode = (len(first) > 0, len(final) > 0)
+    tab_shape = jax.ShapeDtypeStruct((grid, grid, 2 * TILE), BF16)
+    yt_shape = jax.ShapeDtypeStruct((grid, 2 * LINES, TILE), F32)
+    args = [vec, rows, cols, kern, *first, *tables, *final]
+    specs = [IN_VMEM] * 3 + [IN_HBM] + [IN_VMEM] * len(first)
+    if tables:
+        specs += [IN_VMEM, IN_HBM, IN_HBM]
+    if final:
+        specs += [IN_SMEM] * 2 + [IN_VMEM] * (len(final) - 2)
+    out_rows = 3 * blocks + (ROWS if final else 0)
+    shapes = [jax.ShapeDtypeStruct((parts, out_rows, TILE), F32)]
+    out_specs = [IN_VMEM]
+    scratch = [
+        pltpu.VMEM(tab_shape.shape, BF16),
+        pltpu.SemaphoreType.DMA((parts,)),
+        pltpu.VMEM(yt_shape.shape, F32),
+        pltpu.SemaphoreType.DMA((parts,)),
+        pltpu.VMEM(kern.shape, F32),
+        pltpu.SemaphoreType.DMA(()),
+        pltpu.VMEM(((grid + REACH) * LINES, grid), F32),
+    ]
+    if first:
+        shapes += [tab_shape, yt_shape]
+        out_specs += [IN_HBM, IN_HBM]
+    if final:
+        shapes.append(jax.ShapeDtypeStruct((3 * blocks, TILE), F32))
+        out_specs.append(IN_VMEM)
+        scratch += [
+            pltpu.VMEM((blocks + 2 * HALO_BLK, ROWS, TILE), F32),
+            pltpu.VMEM((blocks * TILE, ROWS), F32),
+            pltpu.VMEM((blocks * TILE, ROWS), F32),
+        ]
     return pl.pallas_call(
-        lambda *refs: field_kernel(len(known) > 0, *refs),
+        lambda *refs: field_kernel(mode, *refs),
         in_specs=specs,
-        out_specs=IN_VMEM,
-        out_shape=jax.ShapeDtypeStruct((parts, out_rows, TILE), F32),
-        scratch_shapes=[
-            pltpu.VMEM(table.shape, BF16),
-            pltpu.SemaphoreType.DMA((parts,)),
-            pltpu.VMEM(yt.shape, F32),
-            pltpu.SemaphoreType.DMA((parts,)),
-            pltpu.VMEM(kern.shape, F32),
-            pltpu.SemaphoreType.DMA(()),
-            pltpu.VMEM(((grid + REACH) * LINES, grid), F32),
-        ],
+        out_specs=out_specs,
+        out_shape=shapes,
+        scratch_shapes=scratch,
         name="field",
         **params(1 << 31, 56 << 20),
     )(*args)
 
 
-def pair_kernel(list_ref, count_ref, rank_ref, left_ref, pos_ref, right_ref, col_ref, vec_ref, out_ref, acc_ref, near_ref):
+def pair_kernel(list_ref, count_ref, rank_ref, left_ref, pos_ref, right_ref, vec_ref, out_ref, acc_ref, near_ref, col_ref):
     blocks = pos_ref.shape[1] // TILE
-    ext = blocks + 2 * HALO_BLK
-    total = vec_ref.shape[0] * blocks
+    near_tiles((rank_ref, left_ref, pos_ref, right_ref), vec_ref, near_ref, col_ref)
     chunk = TILE // 2
-    shift = 1.0 * blocks
-    for c in range(3):
-        for j in range(ext):
-            if j < HALO_BLK:
-                row = left_ref[c : c + 1, j * TILE : (j + 1) * TILE] - (shift if c == 0 else 0.0)
-            elif j < HALO_BLK + blocks:
-                i = j - HALO_BLK
-                row = pos_ref[c : c + 1, i * TILE : (i + 1) * TILE]
-            else:
-                i = j - HALO_BLK - blocks
-                row = right_ref[c : c + 1, i * TILE : (i + 1) * TILE] + (shift if c == 0 else 0.0)
-            near_ref[j, c : c + 1, :] = row
-            g = lax.rem(rank_ref[0] * blocks + (j - HALO_BLK) + total, total)
-            src = lax.div(g, blocks)
-            near_ref[j, 3 + c : 4 + c, :] = vec_ref[src, pl.ds(c * blocks + g - src * blocks, 1), :]
-
     shape = (chunk, TILE)
     ahead = lax.broadcasted_iota(jnp.int32, shape, 1) - lax.broadcasted_iota(jnp.int32, shape, 0)
 
@@ -670,20 +736,22 @@
     lax.fori_loop(0, blocks, one_block, 0)
 
 
-def pair_call(tiles, counts, rank, left, pos, right, cols, vec):
+def pair_call(tiles, counts, places, vec):
+    rank, left, pos, right = places
     blocks = pos.shape[1] // TILE
     return pl.pallas_call(
         pair_kernel,
-        in_specs=[IN_SMEM] * 3 + [IN_VMEM] * 5,
+        in_specs=[IN_SMEM] * 3 + [IN_VMEM] * 4,
         out_specs=IN_VMEM,
         out_shape=jax.ShapeDtypeStruct((3 * blocks, TILE), F32),
         scratch_shapes=[
             pltpu.VMEM((3, TILE, TILE), F32),
             pltpu.VMEM((blocks + 2 * HALO_BLK, ROWS, TILE), F32),
+            pltpu.VMEM((blocks * TILE, ROWS), F32),
         ],
         name="pair",
         **params(1 << 30),
-    )(tiles, counts, rank, left, pos, right, cols, vec)
+    )(tiles, counts, rank, left, pos, right, vec)
 
 
 def update_kernel(ret_ref, pair_ref, inv_ref, own_ref, out_ref):
@@ -793,10 +861,15 @@
         field, inv_polar[None, :], x_spline.transpose(1, 0, 2), yz_spline, parts
     )
     everyone = swap(packed)
-    places, everyone = lax.optimization_barrier((positions, everyone))
-    left = lax.ppermute(places[:, atoms - halo :], "gx", up)
-    right = lax.ppermute(places[:, :halo], "gx", down)
-    home_cols = jnp.pad(positions, ((0, ROWS - 3), (0, 0))).T
+    edges, everyone = lax.optimization_barrier((positions, everyone))
+    left = lax.ppermute(edges[:, atoms - halo :], "gx", up)
+    right = lax.ppermute(edges[:, :halo], "gx", down)
+
+    offsets = jnp.arange(SPAN, dtype=jnp.int32)
+    block_ids = jnp.arange(blocks, dtype=jnp.int32)
+    live = jnp.arange(tile_list.shape[1], dtype=jnp.int32)[None, :] < tile_count[:, None]
+    hit = tile_list[:, :, None] == block_ids[:, None, None] + offsets[None, None, :]
+    wts = jnp.sum((hit & live[:, :, None]).astype(F32), axis=1).reshape(-1)
 
     matrix = fourier_matrix(GRID)
     rows, cols = jnp.asarray(matrix), jnp.asarray(matrix.T)
@@ -828,15 +901,20 @@
     turns = jnp.concatenate([ky_modes[None], sine[None], jnp.cos(angle), jnp.sin(angle)])
     turns = jnp.pad(turns.T, ((0, 0), (0, TILE - turns.shape[0])))
 
-    table, yt = prep_call(everyone, z_rows, turns, blocks)
+    partial, table, yt = field_call(everyone, rows, cols, kern, first=(z_rows, turns))
+    tables = (everyone, table, yt)
+    places = (rank[None].astype(jnp.int32), left, positions, right)
     vec, vectors = everyone, [own]
-    rank_id = rank[None].astype(jnp.int32)
     for step in range(ITERS):
         last = step + 1 == ITERS
-        pair = pair_call(tile_list, tile_count, rank_id, left, positions, right, home_cols, vec)
-        known = (*vectors, inv, pair) if last else ()
-        returned = swap(field_call(vec, everyone, table, yt, rows, cols, kern, known))
+        if last:
+            final = (wts, *places, *vectors, inv)
+            partial, pair = field_call(vec, rows, cols, kern, tables=tables, final=final)
+        elif step > 0:
+            (partial,) = field_call(vec, rows, cols, kern, tables=tables)
+        returned = swap(partial)
         if not last:
+            pair = pair_call(tile_list, tile_count, places, vec)
             own, packed = update_call(returned, pair, inv)
             vectors.append(own)
             vec = swap(packed)
@@ -854,6 +932,9 @@
         and planes == ROWS
         and atoms >= HALO_BLK * TILE
         and ORDER == 5
+        and atoms % parts == 0
+        and (atoms // parts) % 32 == 0
+        and TILE % (atoms // parts) == 0
         and ITERS == 3
     )
     run = per_device_modes if modes else per_device_general

time: 173 us -> 164 us (0.948)
  blocking collectives: 41.8 us -> 27.4 us
  waiting for transfers between devices: 14.7 us -> 23.9 us
  Pallas kernels: 88.2 us -> 79.9 us
  starting transfers between devices: 18.8 us -> 24.2 us
    all_to_all x3 -> x2, blocking collectives: 41.8 us -> 27.4 us  [swap(): return lax.all_to_all(x, 'gx', split_axis=0, concat_axis=0, tiled=True)]
    all_to_all x3 -> x4, waiting for transfers between devices: 9.81 us -> 18.2 us  [swap(): return lax.all_to_all(x, 'gx', split_axis=0, concat_axis=0, tiled=True)]
    pallas_call x7 -> x5, Pallas kernels: 80 us -> 71.6 us  [the longest x3 56.2 us: field_call(): pl.pallas_call(lambda *refs: field_kernel(mode, *refs), in_specs=specs, o...]
    all_to_all x3 -> x4, starting transfers between devices: 14.5 us -> 19.8 us  [swap(): return lax.all_to_all(x, 'gx', split_axis=0, concat_axis=0, tiled=True)]
    unnamed x15 -> x21, local copies, waits for them, and re-layouts: 2.94 us -> 3.46 us
  transfers between devices with their start and end apart: 5 -> 6, of which waited for: 4 -> 5; matrix products, arithmetic and copies ran while one was open for 3% -> 2% of each run, Pallas kernels for 9% -> 9%
where the time goes in v2:
time: 164 us
  Pallas kernels  79.9 us (49%)
  blocking collectives  27.4 us (17%)
  starting transfers between devices  24.2 us (15%)
  waiting for transfers between devices  23.9 us (15%)
  local copies, waits for them, and re-layouts  5.9 us (4%)
    pallas_call x3, Pallas kernels, field_call(): pl.pallas_call(lambda *refs: field_kernel(mode, *refs), in_specs=specs, o...  56.2 us
    all_to_all x2, blocking collectives, swap(): return lax.all_to_all(x, 'gx', split_axis=0, concat_axis=0, tiled=True)  27.4 us
    all_to_all x4, starting transfers between devices, swap(): return lax.all_to_all(x, 'gx', split_axis=0, concat_axis=0, tiled=True)  19.8 us
    all_to_all x4, waiting for transfers between devices, swap(): return lax.all_to_all(x, 'gx', split_axis=0, concat_axis=0, tiled=True)  18.2 us
    pallas_call x2, Pallas kernels, pair_call(): pl.pallas_call(pair_kernel, in_specs=[IN_SMEM] * 3 + [IN_VMEM] * 4, out_s...  15.4 us
    ppermute x1, waiting for transfers between devices, per_device_modes(): left = lax.ppermute(edges[:, atoms - halo:], 'gx', up)  4.4 us
    ppermute x1, starting transfers between devices, per_device_modes(): right = lax.ppermute(edges[:, :halo], 'gx', down)  4.37 us
    unnamed x21, local copies, waits for them, and re-layouts  3.46 us
  transfers between devices with their start and end apart: 6, of which 5 were waited for; matrix products, arithmetic and copies ran while one was open for 2% of the time, Pallas kernels for 9%

profile of v2, /device:TPU:0, one launch (start us, length us, event | category | flops | bytes accessed | tf_op | source)
XLA Modules:
  0.0 163.6 jit_solution(7230251919857675451)
XLA Ops:
  0.6 3.1 %pack.1 = (f32[24,128]{1,0:T(8,128)}, f32[8,128]{1,0:T(8,128)}, f32[16,48,128]{2,1,0:T(8,128)}) custom-call(f32[3,1024]{1,0:T(4,128)} %field_ref.1, f32[1,1024]{1,0:T(1,128)} %bitcast.14, f32[5,2,1024]{2,1,0:T(2,128)} %bitcast.13, f32[4,1024,128]{2,1,0:T(8,128)} %yz_ref.1), custom_call_target="tpu_custom_call" | custom-call | flops 67108864 | bytes 4194304 | tf_op jit(solution)/shard_map/pack/pallas_call | solution.py:334
  3.8 7.4 %all-to-all-start = ((f32[16,48,128]{2,1,0:T(8,128)}), f32[16,48,128]{2,1,0:T(8,128)S(1)}, u32[]{:S(2)}, u32[]{:S(2)}) async-start(f32[16,48,128]{2,1,0:T(8,128)} %get-tuple-element.16), calls=%async_computation | async-start | bytes 786432 | tf_op jit(solution)/shard_map/all_to_all | solution.py:848
  13.3 1.2 fusion.2.refs_3_
  14.5 8.8 %all-to-all-done.refs_0_.vec_ref.refs_4_ = f32[16,48,128]{2,1,0:T(8,128)S(1)} async-done(((f32[16,48,128]{2,1,0:T(8,128)}), f32[16,48,128]{2,1,0:T(8,128)S(1)}, u32[]{:S(2)}, u32[]{:S(2)}) %all-to-all-start) | async-done | bytes 393248 | tf_op jit(solution)/shard_map/all_to_all | solution.py:848
  23.3 0.7 copy-done
  24.1 23.6 %field.3 = (f32[16,24,128]{2,1,0:T(8,128)}, bf16[128,128,256]{2,1,0:T(8,128)(2,1)}, f32[128,32,128]{2,1,0:T(8,128)}) custom-call(f32[16,48,128]{2,1,0:T(8,128)} %copy-done, f32[128,128]{1,0:T(8,128)} %constant.71.clone.refs_1_, f32[128,128]{1,0:T(8,128)} %constant.72.clone.refs_2_, f32[128,1024]{1,0:T(8,128)} %fusion.2.refs_3_, ...), custom_call_target="tpu_custom_call" | custom-call | flops 2147483648 | bytes 4194304 | tf_op jit(solution)/shard_map/field/pallas_call | solution.py:686
  47.7 3.5 %all-to-all-start.1 = ((f32[16,24,128]{2,1,0:T(8,128)}), f32[16,24,128]{2,1,0:T(8,128)S(1)}, u32[]{:S(2)}, u32[]{:S(2)}) async-start(f32[16,24,128]{2,1,0:T(8,128)} %get-tuple-element.18), calls=%async_computation.1 | async-start | bytes 393216 | tf_op jit(solution)/shard_map/all_to_all | solution.py:848
  51.2 4.4 %collective-permute-start.1 = (f32[3,384]{1,0:T(4,128)S(1)}, f32[3,384]{1,0:T(4,128)S(1)}, u32[]{:S(2)}, u32[]{:S(2)}) collective-permute-start(f32[3,384]{1,0:T(4,128)S(1)} %get-tuple-element.30), channel_id=1, source_target_pairs={{1,0},{2,1},{3,2},{4,3},{5,4},{6,5},{7,6},{8,7},{9,8},{10,9},{11,1... | collective-permute-start | bytes 13832 | tf_op jit(solution)/shard_map/ppermute | solution.py:866
  55.6 1.3 collective-permute-done.1.right_ref.refs_11_
  57.0 4.4 %collective-permute-done.left_ref.refs_9_ = f32[3,384]{1,0:T(4,128)S(1)} collective-permute-done((f32[3,384]{1,0:T(4,128)S(1)}, f32[3,384]{1,0:T(4,128)S(1)}, u32[]{:S(2)}, u32[]{:S(2)}) %collective-permute-start) | collective-permute-done | bytes 4640 | tf_op jit(solution)/shard_map/ppermute | solution.py:865
  62.0 7.8 %pair.2.pair_ref = f32[24,128]{1,0:T(8,128)} custom-call(s32[8,7]{1,0:T(8,128)} %list_ref.3, s32[8]{0:T(128)} %count_ref.3, s32[1]{0:T(128)} %bitcast.7.rank_ref.refs_8_, f32[3,384]{1,0:T(4,128)} %copy-done.7, f32[3,1024]{1,0:T(4,128)} %refs_10_.1, f32[3,384]{1,0:T(4,128)} %copy-done.6, f32[16,48,128]{2,1,0:T(8,128)} %copy-done), custom_call_target="tpu_custom_call" | custom-call | flops 1073741824 | bytes 4194304 | tf_op jit(solution)/shard_map/pair/pallas_call | solution.py:742
  69.7 0.7 copy-done.1
  70.4 1.7 %update.2 = (f32[24,128]{1,0:T(8,128)}, f32[16,24,128]{2,1,0:T(8,128)}) custom-call(f32[16,24,128]{2,1,0:T(8,128)} %copy-done.1, f32[24,128]{1,0:T(8,128)} %pair.2.pair_ref, f32[8,128]{1,0:T(8,128)} %get-tuple-element.20.inv_ref.refs_15_), custom_call_target="tpu_custom_call" | custom-call | flops 16777216 | bytes 4194304 | tf_op jit(solution)/shard_map/update/pallas_call | solution.py:769
  72.0 13.1 %all_to_all.30.refs_0_.vec_ref = f32[16,24,128]{2,1,0:T(8,128)} all-to-all(f32[16,24,128]{2,1,0:T(8,128)} %get-tuple-element.21), channel_id=1, replica_groups=mesh['rep'=2,'gx'=16] {'gx'}, dimensions={0} | all-to-all | bytes 393216 | tf_op jit(solution)/shard_map/all_to_all | solution.py:848
  85.2 14.4 %field.4 = f32[16,24,128]{2,1,0:T(8,128)} custom-call(f32[16,24,128]{2,1,0:T(8,128)} %all_to_all.30.refs_0_.vec_ref, f32[128,128]{1,0:T(8,128)} %constant.71.clone.refs_1_, f32[128,128]{1,0:T(8,128)} %constant.72.clone.refs_2_, f32[128,1024]{1,0:T(8,128)} %fusion.2.refs_3_, f32[16,48,128]{2,1,0:T(8,128)} %copy-done, ...), custom_call_target="tpu_custom_call" | custom-call | flops 2147483648 | bytes 4194304 | tf_op jit(solution)/shard_map/field/pallas_call | solution.py:686
  99.6 3.5 %all-to-all-start.3 = ((f32[16,24,128]{2,1,0:T(8,128)}), f32[16,24,128]{2,1,0:T(8,128)S(1)}, u32[]{:S(2)}, u32[]{:S(2)}) async-start(f32[16,24,128]{2,1,0:T(8,128)} %field.4), calls=%async_computation.3 | async-start | bytes 393216 | tf_op jit(solution)/shard_map/all_to_all | solution.py:848
  103.1 7.7 %pair.3.pair_ref = f32[24,128]{1,0:T(8,128)} custom-call(s32[8,7]{1,0:T(8,128)} %list_ref.3, s32[8]{0:T(128)} %count_ref.3, s32[1]{0:T(128)} %bitcast.7.rank_ref.refs_8_, f32[3,384]{1,0:T(4,128)} %copy-done.7, f32[3,1024]{1,0:T(4,128)} %refs_10_.1, f32[3,384]{1,0:T(4,128)} %copy-done.6, f32[16,24,128]{2,1,0:T(8,128)} %all_to_all.30.refs_0_.vec_ref), custom_call_target="tpu_custom_call" | custom-call | flops 1073741824 | bytes 4194304 | tf_op jit(solution)/shard_map/pair/pallas_call | solution.py:742
  110.8 1.2 all-to-all-done.3.ret_ref
  112.7 1.7 %update.3 = (f32[24,128]{1,0:T(8,128)}, f32[16,24,128]{2,1,0:T(8,128)}) custom-call(f32[16,24,128]{2,1,0:T(8,128)} %copy-done.2, f32[24,128]{1,0:T(8,128)} %pair.3.pair_ref, f32[8,128]{1,0:T(8,128)} %get-tuple-element.20.inv_ref.refs_15_), custom_call_target="tpu_custom_call" | custom-call | flops 16777216 | bytes 4194304 | tf_op jit(solution)/shard_map/update/pallas_call | solution.py:769
  114.4 5.3 %all-to-all-start.4 = ((f32[16,24,128]{2,1,0:T(8,128)}), f32[16,24,128]{2,1,0:T(8,128)S(1)}, u32[]{:S(2)}, u32[]{:S(2)}) async-start(f32[16,24,128]{2,1,0:T(8,128)} %get-tuple-element.24), calls=%async_computation.4 | async-start | bytes 393216 | tf_op jit(solution)/shard_map/all_to_all | solution.py:848
  120.5 8.2 %all-to-all-done.4.refs_0_ = f32[16,24,128]{2,1,0:T(8,128)S(1)} async-done(((f32[16,24,128]{2,1,0:T(8,128)}), f32[16,24,128]{2,1,0:T(8,128)S(1)}, u32[]{:S(2)}, u32[]{:S(2)}) %all-to-all-start.4) | async-done | bytes 196640 | tf_op jit(solution)/shard_map/all_to_all | solution.py:848
  129.4 18.2 %field.5 = (f32[16,32,128]{2,1,0:T(8,128)}, f32[24,128]{1,0:T(8,128)}) custom-call(f32[16,24,128]{2,1,0:T(8,128)} %copy-done.3, f32[128,128]{1,0:T(8,128)} %constant.71.clone.refs_1_, f32[128,128]{1,0:T(8,128)} %constant.72.clone.refs_2_, f32[128,1024]{1,0:T(8,128)} %fusion.2.refs_3_, f32[16,48,128]{2,1,0:T(8,128)} %copy-done, ...), custom_call_target="tpu_custom_call" | custom-call | flops 2147483648 | bytes 4194304 | tf_op jit(solution)/shard_map/field/pallas_call | solution.py:686
  147.6 14.2 %all_to_all.31.ret_ref = f32[16,32,128]{2,1,0:T(8,128)} all-to-all(f32[16,32,128]{2,1,0:T(8,128)} %get-tuple-element.28), channel_id=1, replica_groups=mesh['rep'=2,'gx'=16] {'gx'}, dimensions={0} | all-to-all | bytes 524288 | tf_op jit(solution)/shard_map/all_to_all | solution.py:848
  161.8 1.8 %finish.1 = (f32[3,1024]{1,0:T(4,128)}, f32[3,1024]{1,0:T(4,128)}) custom-call(f32[16,32,128]{2,1,0:T(8,128)} %all_to_all.31.ret_ref, f32[24,128]{1,0:T(8,128)} %get-tuple-element.29.pair_ref, f32[24,128]{1,0:T(8,128)} %get-tuple-element.25.refs_12_.v0_ref, f32[24,128]{1,0:T(8,128)} %get-tuple-element.26.refs_13_.v1_ref, ...), custom_call_target="tpu_custom_call" | custom-call | flops 16777216 | bytes 4194304 | tf_op jit(solution)/shard_map/finish/pallas_call | solution.py:822
  (47 shorter events, 4.8 us)
Async XLA Ops:
  0.6 12.1 %copy-start.4 = (f32[128,128]{1,0:T(8,128)S(1)}, f32[128,128]{1,0:T(8,128)}, u32[]{:S(2)}) copy-start(f32[128,128]{1,0:T(8,128)} %constant.71.clone.refs_1_) | copy-start | bytes 196612
  3.8 19.6 %all-to-all-start = ((f32[16,48,128]{2,1,0:T(8,128)}), f32[16,48,128]{2,1,0:T(8,128)S(1)}, u32[]{:S(2)}, u32[]{:S(2)}) async-start(f32[16,48,128]{2,1,0:T(8,128)} %get-tuple-element.16), calls=%async_computation | async-start | bytes 786432 | tf_op jit(solution)/shard_map/all_to_all | solution.py:848
  14.5 36.7 %copy-start.5 = (f32[3,1024]{1,0:T(4,128)S(1)}, f32[3,1024]{1,0:T(4,128)}, u32[]{:S(2)}) copy-start(f32[3,1024]{1,0:T(4,128)} %refs_10_.1) | copy-start | bytes 36868
  23.3 0.7 copy-start
  47.7 22.0 %all-to-all-start.1 = ((f32[16,24,128]{2,1,0:T(8,128)}), f32[16,24,128]{2,1,0:T(8,128)S(1)}, u32[]{:S(2)}, u32[]{:S(2)}) async-start(f32[16,24,128]{2,1,0:T(8,128)} %get-tuple-element.18), calls=%async_computation.1 | async-start | bytes 393216 | tf_op jit(solution)/shard_map/all_to_all | solution.py:848
  51.2 5.7 %collective-permute-start.1 = (f32[3,384]{1,0:T(4,128)S(1)}, f32[3,384]{1,0:T(4,128)S(1)}, u32[]{:S(2)}, u32[]{:S(2)}) collective-permute-start(f32[3,384]{1,0:T(4,128)S(1)} %get-tuple-element.30), channel_id=1, source_target_pairs={{1,0},{2,1},{3,2},{4,3},{5,4},{6,5},{7,6},{8,7},{9,8},{10,9},{11,1... | collective-permute-start | bytes 13832 | tf_op jit(solution)/shard_map/ppermute | solution.py:866
  55.6 5.8 %collective-permute-start = (f32[3,384]{1,0:T(4,128)S(1)}, f32[3,384]{1,0:T(4,128)S(1)}, u32[]{:S(2)}, u32[]{:S(2)}) collective-permute-start(f32[3,384]{1,0:T(4,128)S(1)} %get-tuple-element.31), channel_id=1, source_target_pairs={{0,1},{1,2},{2,3},{3,4},{4,5},{5,6},{6,7},{7,8},{8,9},{9,10},{10,1... | collective-permute-start | bytes 13832 | tf_op jit(solution)/shard_map/ppermute | solution.py:865
  57.0 4.4 %copy-start.6 = (f32[3,384]{1,0:T(4,128)}, f32[3,384]{1,0:T(4,128)S(1)}, u32[]{:S(2)}) copy-start(f32[3,384]{1,0:T(4,128)S(1)} %collective-permute-done.1.right_ref.refs_11_) | copy-start | bytes 13828
  61.4 0.6 copy-start.7
  69.7 0.7 copy-start.1
  99.6 12.5 %all-to-all-start.3 = ((f32[16,24,128]{2,1,0:T(8,128)}), f32[16,24,128]{2,1,0:T(8,128)S(1)}, u32[]{:S(2)}, u32[]{:S(2)}) async-start(f32[16,24,128]{2,1,0:T(8,128)} %field.4), calls=%async_computation.3 | async-start | bytes 393216 | tf_op jit(solution)/shard_map/all_to_all | solution.py:848
  103.1 16.6 %copy-start.8 = (s32[8,7]{1,0:T(8,128)S(1)}, s32[8,7]{1,0:T(8,128)}, u32[]{:S(2)}) copy-start(s32[8,7]{1,0:T(8,128)} %list_ref.3) | copy-start | bytes 676
  103.1 16.7 %copy-start.9 = (s32[8]{0:T(128)S(1)}, s32[8]{0:T(128)}, u32[]{:S(2)}) copy-start(s32[8]{0:T(128)} %count_ref.3) | copy-start | bytes 100
  112.1 0.7 copy-start.2
  114.4 14.3 %all-to-all-start.4 = ((f32[16,24,128]{2,1,0:T(8,128)}), f32[16,24,128]{2,1,0:T(8,128)S(1)}, u32[]{:S(2)}, u32[]{:S(2)}) async-start(f32[16,24,128]{2,1,0:T(8,128)} %get-tuple-element.24), calls=%async_computation.4 | async-start | bytes 393216 | tf_op jit(solution)/shard_map/all_to_all | solution.py:848
  128.7 0.7 copy-start.3

commit v3 on v2

--- a/solution.py
+++ b/solution.py
@@ -251,6 +251,10 @@
 SPAN = 2 * HALO_BLK + 1
 PACKED = 6
 NT = (((1,), (1,)), ((), ()))
+
+
+def near(x):
+    return pltpu.with_memory_space_constraint(x, pltpu.VMEM)
 
 
 def params(flops, vmem=None):
@@ -336,9 +340,9 @@
         in_specs=[IN_VMEM] * 4,
         out_specs=[IN_VMEM] * 3,
         out_shape=[
-            jax.ShapeDtypeStruct((3 * blocks, TILE), F32),
-            jax.ShapeDtypeStruct((blocks, TILE), F32),
-            jax.ShapeDtypeStruct((parts, PACKED * blocks, TILE), F32),
+            pltpu.VMEM((3 * blocks, TILE), F32),
+            pltpu.VMEM((blocks, TILE), F32),
+            pltpu.VMEM((parts, PACKED * blocks, TILE), F32),
         ],
         name="pack",
         **params(1 << 26),
@@ -455,9 +459,9 @@
         hz = jnp.broadcast_to(home[:, 2:3], shape)
         sx = sy = sz = jnp.zeros(shape, F32)
         for e in range(SPAN):
-            near = near_ref[b + e]
-            dx, dy, dz = hx - near[0:1], hy - near[1:2], hz - near[2:3]
-            vx, vy, vz = near[3:4], near[4:5], near[5:6]
+            tile = near_ref[b + e]
+            dx, dy, dz = hx - tile[0:1], hy - tile[1:2], hz - tile[2:3]
+            vx, vy, vz = tile[3:4], tile[4:5], tile[5:6]
             inverse = lax.rsqrt(dx * dx + dy * dy + dz * dz + 1.0)
             square = inverse * inverse
             third = wts_ref[b * SPAN + e] * (inverse * square)
@@ -654,14 +658,15 @@
     mode = (len(first) > 0, len(final) > 0)
     tab_shape = jax.ShapeDtypeStruct((grid, grid, 2 * TILE), BF16)
     yt_shape = jax.ShapeDtypeStruct((grid, 2 * LINES, TILE), F32)
-    args = [vec, rows, cols, kern, *first, *tables, *final]
+    tables = [near(tables[0]), *tables[1:]] if tables else []
+    args = [near(vec), rows, cols, kern, *first, *tables, *final[:5], *map(near, final[5:])]
     specs = [IN_VMEM] * 3 + [IN_HBM] + [IN_VMEM] * len(first)
     if tables:
         specs += [IN_VMEM, IN_HBM, IN_HBM]
     if final:
         specs += [IN_SMEM] * 2 + [IN_VMEM] * (len(final) - 2)
     out_rows = 3 * blocks + (ROWS if final else 0)
-    shapes = [jax.ShapeDtypeStruct((parts, out_rows, TILE), F32)]
+    shapes = [pltpu.VMEM((parts, out_rows, TILE), F32)]
     out_specs = [IN_VMEM]
     scratch = [
         pltpu.VMEM(tab_shape.shape, BF16),
@@ -676,7 +681,7 @@
         shapes += [tab_shape, yt_shape]
         out_specs += [IN_HBM, IN_HBM]
     if final:
-        shapes.append(jax.ShapeDtypeStruct((3 * blocks, TILE), F32))
+        shapes.append(pltpu.VMEM((3 * blocks, TILE), F32))
         out_specs.append(IN_VMEM)
         scratch += [
             pltpu.VMEM((blocks + 2 * HALO_BLK, ROWS, TILE), F32),
@@ -711,9 +716,9 @@
             def one_tile(k, sums):
                 sx, sy, sz = sums
                 j = list_ref[b, k]
-                near = near_ref[j]
-                dx, dy, dz = hx - near[0:1], hy - near[1:2], hz - near[2:3]
-                vx, vy, vz = near[3:4], near[4:5], near[5:6]
+                tile = near_ref[j]
+                dx, dy, dz = hx - tile[0:1], hy - tile[1:2], hz - tile[2:3]
+                vx, vy, vz = tile[3:4], tile[4:5], tile[5:6]
                 inverse = lax.rsqrt(dx * dx + dy * dy + dz * dz + 1.0)
                 square = inverse * inverse
                 itself = ahead == c * chunk - (j - b - HALO_BLK) * TILE
@@ -743,7 +748,7 @@
         pair_kernel,
         in_specs=[IN_SMEM] * 3 + [IN_VMEM] * 4,
         out_specs=IN_VMEM,
-        out_shape=jax.ShapeDtypeStruct((3 * blocks, TILE), F32),
+        out_shape=pltpu.VMEM((3 * blocks, TILE), F32),
         scratch_shapes=[
             pltpu.VMEM((3, TILE, TILE), F32),
             pltpu.VMEM((blocks + 2 * HALO_BLK, ROWS, TILE), F32),
@@ -751,7 +756,7 @@
         ],
         name="pair",
         **params(1 << 30),
-    )(tiles, counts, rank, left, pos, right, vec)
+    )(tiles, counts, rank, left, pos, right, near(vec))
 
 
 def update_kernel(ret_ref, pair_ref, inv_ref, own_ref, out_ref):
@@ -771,12 +776,12 @@
         in_specs=[IN_VMEM] * 3,
         out_specs=[IN_VMEM] * 2,
         out_shape=[
-            jax.ShapeDtypeStruct(pair.shape, F32),
-            jax.ShapeDtypeStruct((parts,) + pair.shape, F32),
+            pltpu.VMEM(pair.shape, F32),
+            pltpu.VMEM((parts,) + pair.shape, F32),
         ],
         name="update",
         **params(1 << 24),
-    )(returned, pair, inv)
+    )(near(returned), near(pair), near(inv))
 
 
 def finish_kernel(ret_ref, pair_ref, v0_ref, v1_ref, v2_ref, inv_ref, dip_ref, res_ref):
@@ -826,7 +831,7 @@
         out_shape=[jax.ShapeDtypeStruct((3, atoms), F32)] * 2,
         name="finish",
         **params(1 << 24),
-    )(returned, pair, *vectors, inv)
+    )(*map(near, (returned, pair, *vectors, inv)))
 
 
 def fourier_matrix(size):

time: 164 us -> 152 us (0.927)
  Pallas kernels: 79.9 us -> 73.4 us
  blocking collectives: 27.4 us -> 24.2 us
  local copies, waits for them, and re-layouts: 5.9 us -> 3.14 us
    all_to_all x2, blocking collectives: 27.4 us -> 24.2 us  [swap(): return lax.all_to_all(x, 'gx', split_axis=0, concat_axis=0, tiled=True)]
    unnamed x21 -> x13, local copies, waits for them, and re-layouts: 3.46 us -> 0.7 us
    pallas_call x2, Pallas kernels: 3.31 us -> 0.74 us  [update_call(): pl.pallas_call(update_kernel, in_specs=[IN_VMEM] * 3, out_specs=[IN_VMEM]...]
  transfers between devices with their start and end apart: 6 -> 6, of which waited for: 5 -> 5; matrix products, arithmetic and copies ran while one was open for 2% -> 3% of each run, Pallas kernels for 9% -> 9%
where the time goes in v3:
time: 152 us; the launch traced here: 151 us
  Pallas kernels  73.4 us (48%)
  waiting for transfers between devices  24.7 us (16%)
  blocking collectives  24.2 us (16%)
  starting transfers between devices  23.4 us (15%)
  local copies, waits for them, and re-layouts  3.14 us (2%)
    pallas_call x3, Pallas kernels, field_call(): pl.pallas_call(lambda *refs: field_kernel(mode, *refs), in_specs=specs, o...  54.8 us
    all_to_all x2, blocking collectives, swap(): return lax.all_to_all(x, 'gx', split_axis=0, concat_axis=0, tiled=True)  24.2 us
    all_to_all x4, starting transfers between devices, swap(): return lax.all_to_all(x, 'gx', split_axis=0, concat_axis=0, tiled=True)  19.1 us
    all_to_all x4, waiting for transfers between devices, swap(): return lax.all_to_all(x, 'gx', split_axis=0, concat_axis=0, tiled=True)  18.9 us
    pallas_call x2, Pallas kernels, pair_call(): pl.pallas_call(pair_kernel, in_specs=[IN_SMEM] * 3 + [IN_VMEM] * 4, out_s...  13.9 us
    ppermute x1, waiting for transfers between devices, per_device_modes(): left = lax.ppermute(edges[:, atoms - halo:], 'gx', up)  4.4 us
    ppermute x1, starting transfers between devices, per_device_modes(): right = lax.ppermute(edges[:, :halo], 'gx', down)  4.37 us
    pallas_call x1, Pallas kernels, pack_call(): pl.pallas_call(pack_kernel, in_specs=[IN_VMEM] * 4, out_specs=[IN_VMEM] *...  3.13 us
  transfers between devices with their start and end apart: 6, of which 5 were waited for; matrix products, arithmetic and copies ran while one was open for 3% of the time, Pallas kernels for 9%

profile of v3, /device:TPU:0, one launch (start us, length us, event | category | flops | bytes accessed | tf_op | source)
XLA Modules:
  0.0 151.2 jit_solution(8443194083071986290)
XLA Ops:
  0.6 3.1 %pack.1 = (f32[24,128]{1,0:T(8,128)S(1)}, f32[8,128]{1,0:T(8,128)S(1)}, f32[16,48,128]{2,1,0:T(8,128)}) custom-call(f32[3,1024]{1,0:T(4,128)} %field_ref.1, f32[1,1024]{1,0:T(1,128)} %bitcast.14, f32[5,2,1024]{2,1,0:T(2,128)} %bitcast.13, f32[4,1024,128]{2,1,0:T(8,128)} %yz_ref.1), custom_call_target="tpu_custom_call" | custom-call | flops 67108864 | bytes 4194304 | tf_op jit(solution)/shard_map/pack/pallas_call | solution.py:338
  3.8 7.4 %all-to-all-start = ((f32[16,48,128]{2,1,0:T(8,128)}), f32[16,48,128]{2,1,0:T(8,128)S(1)}, u32[]{:S(2)}, u32[]{:S(2)}) async-start(f32[16,48,128]{2,1,0:T(8,128)} %get-tuple-element.16), calls=%async_computation | async-start | bytes 786432 | tf_op jit(solution)/shard_map/all_to_all | solution.py:853
  12.1 0.6 pad.4.refs_5_
  12.7 0.6 constant_dynamic-slice_fusion.refs_4_
  13.3 1.1 fusion.2.refs_3_
  14.5 8.8 %all-to-all-done.refs_0_.vec_ref.refs_4_ = f32[16,48,128]{2,1,0:T(8,128)S(1)} async-done(((f32[16,48,128]{2,1,0:T(8,128)}), f32[16,48,128]{2,1,0:T(8,128)S(1)}, u32[]{:S(2)}, u32[]{:S(2)}) %all-to-all-start) | async-done | bytes 393248 | tf_op jit(solution)/shard_map/all_to_all | solution.py:853
  23.3 23.4 %field.3 = (f32[16,24,128]{2,1,0:T(8,128)}, bf16[128,128,256]{2,1,0:T(8,128)(2,1)}, f32[128,32,128]{2,1,0:T(8,128)}) custom-call(f32[16,48,128]{2,1,0:T(8,128)S(1)} %all-to-all-done.refs_0_.vec_ref.refs_4_, f32[128,128]{1,0:T(8,128)} %constant.71.clone.refs_1_, f32[128,128]{1,0:T(8,128)} %constant.72.clone.refs_2_, f32[128,1024]{1,0:T(8,128)} %fusion.2.refs_3_, ...), custom_call_target="tpu_custom_call" | custom-call | flops 2147483648 | bytes 4194304 | tf_op jit(solution)/shard_map/field/pallas_call | solution.py:691
  46.8 3.5 %all-to-all-start.1 = ((f32[16,24,128]{2,1,0:T(8,128)}), f32[16,24,128]{2,1,0:T(8,128)S(1)}, u32[]{:S(2)}, u32[]{:S(2)}) async-start(f32[16,24,128]{2,1,0:T(8,128)} %get-tuple-element.18), calls=%async_computation.1 | async-start | bytes 393216 | tf_op jit(solution)/shard_map/all_to_all | solution.py:853
  50.3 4.4 %collective-permute-start.1 = (f32[3,384]{1,0:T(4,128)S(1)}, f32[3,384]{1,0:T(4,128)S(1)}, u32[]{:S(2)}, u32[]{:S(2)}) collective-permute-start(f32[3,384]{1,0:T(4,128)S(1)} %get-tuple-element.30), channel_id=1, source_target_pairs={{1,0},{2,1},{3,2},{4,3},{5,4},{6,5},{7,6},{8,7},{9,8},{10,9},{11,1... | collective-permute-start | bytes 13832 | tf_op jit(solution)/shard_map/ppermute | solution.py:871
  54.7 1.3 collective-permute-done.1.right_ref.refs_11_
  56.0 4.4 %collective-permute-done.left_ref.refs_9_ = f32[3,384]{1,0:T(4,128)S(1)} collective-permute-done((f32[3,384]{1,0:T(4,128)S(1)}, f32[3,384]{1,0:T(4,128)S(1)}, u32[]{:S(2)}, u32[]{:S(2)}) %collective-permute-start) | collective-permute-done | bytes 4640 | tf_op jit(solution)/shard_map/ppermute | solution.py:870
  61.0 7.0 %pair.2.pair_ref = f32[24,128]{1,0:T(8,128)S(1)} custom-call(s32[8,7]{1,0:T(8,128)} %list_ref.3, s32[8]{0:T(128)} %count_ref.3, s32[1]{0:T(128)} %bitcast.7.rank_ref.refs_8_, f32[3,384]{1,0:T(4,128)} %copy-done.3, f32[3,1024]{1,0:T(4,128)} %refs_10_.1, f32[3,384]{1,0:T(4,128)} %copy-done.2, f32[16,48,128]{2,1,0:T(8,128)S(1)} %all-to-all-done.refs_0_.vec_ref.refs_4_), custom_call_target="tpu_custom_call" | custom-call | flops 1073741824 | bytes 4194304 | tf_op jit(solution)/shard_map/pair/pallas_call | solution.py:747
  68.1 11.6 %all_to_all.30.refs_0_.vec_ref = f32[16,24,128]{2,1,0:T(8,128)S(1)} all-to-all(f32[16,24,128]{2,1,0:T(8,128)S(1)} %get-tuple-element.21), channel_id=1, replica_groups=mesh['rep'=2,'gx'=16] {'gx'}, dimensions={0} | all-to-all | bytes 393216 | tf_op jit(solution)/shard_map/all_to_all | solution.py:853
  79.6 14.1 %field.4 = f32[16,24,128]{2,1,0:T(8,128)} custom-call(f32[16,24,128]{2,1,0:T(8,128)S(1)} %all_to_all.30.refs_0_.vec_ref, f32[128,128]{1,0:T(8,128)} %constant.71.clone.refs_1_, f32[128,128]{1,0:T(8,128)} %constant.72.clone.refs_2_, f32[128,1024]{1,0:T(8,128)} %fusion.2.refs_3_, f32[16,48,128]{2,1,0:T(8,128)S(1)} %all-to-all-done.refs_0_.vec_ref.refs_4_, ...), custom_call_target="tpu_custom_call" | custom-call | flops 2147483648 | bytes 4194304 | tf_op jit(solution)/shard_map/field/pallas_call | solution.py:691
  93.7 3.5 %all-to-all-start.3 = ((f32[16,24,128]{2,1,0:T(8,128)}), f32[16,24,128]{2,1,0:T(8,128)S(1)}, u32[]{:S(2)}, u32[]{:S(2)}) async-start(f32[16,24,128]{2,1,0:T(8,128)} %field.4), calls=%async_computation.3 | async-start | bytes 393216 | tf_op jit(solution)/shard_map/all_to_all | solution.py:853
  97.3 7.0 %pair.3.pair_ref = f32[24,128]{1,0:T(8,128)S(1)} custom-call(s32[8,7]{1,0:T(8,128)} %list_ref.3, s32[8]{0:T(128)} %count_ref.3, s32[1]{0:T(128)} %bitcast.7.rank_ref.refs_8_, f32[3,384]{1,0:T(4,128)} %copy-done.3, f32[3,1024]{1,0:T(4,128)} %refs_10_.1, f32[3,384]{1,0:T(4,128)} %copy-done.2, f32[16,24,128]{2,1,0:T(8,128)S(1)} %all_to_all.30.refs_0_.vec_ref), custom_call_target="tpu_custom_call" | custom-call | flops 1073741824 | bytes 4194304 | tf_op jit(solution)/shard_map/pair/pallas_call | solution.py:747
  104.2 1.9 %all-to-all-done.3.ret_ref = f32[16,24,128]{2,1,0:T(8,128)S(1)} async-done(((f32[16,24,128]{2,1,0:T(8,128)}), f32[16,24,128]{2,1,0:T(8,128)S(1)}, u32[]{:S(2)}, u32[]{:S(2)}) %all-to-all-start.3) | async-done | bytes 196640 | tf_op jit(solution)/shard_map/all_to_all | solution.py:853
  106.2 0.7 update.3
  106.9 4.6 %all-to-all-start.4 = ((f32[16,24,128]{2,1,0:T(8,128)}), f32[16,24,128]{2,1,0:T(8,128)S(1)}, u32[]{:S(2)}, u32[]{:S(2)}) async-start(f32[16,24,128]{2,1,0:T(8,128)} %get-tuple-element.24), calls=%async_computation.4 | async-start | bytes 393216 | tf_op jit(solution)/shard_map/all_to_all | solution.py:853
  111.7 0.6 reshape.190.refs_7_
  112.3 8.2 %all-to-all-done.4.refs_0_ = f32[16,24,128]{2,1,0:T(8,128)S(1)} async-done(((f32[16,24,128]{2,1,0:T(8,128)}), f32[16,24,128]{2,1,0:T(8,128)S(1)}, u32[]{:S(2)}, u32[]{:S(2)}) %all-to-all-start.4) | async-done | bytes 196640 | tf_op jit(solution)/shard_map/all_to_all | solution.py:853
  120.5 17.2 %field.5 = (f32[16,32,128]{2,1,0:T(8,128)S(1)}, f32[24,128]{1,0:T(8,128)S(1)}) custom-call(f32[16,24,128]{2,1,0:T(8,128)S(1)} %all-to-all-done.4.refs_0_, f32[128,128]{1,0:T(8,128)} %constant.71.clone.refs_1_, f32[128,128]{1,0:T(8,128)} %constant.72.clone.refs_2_, f32[128,1024]{1,0:T(8,128)} %fusion.2.refs_3_, ...), custom_call_target="tpu_custom_call" | custom-call | flops 2147483648 | bytes 4194304 | tf_op jit(solution)/shard_map/field/pallas_call | solution.py:691
  137.7 12.6 %all_to_all.31.ret_ref = f32[16,32,128]{2,1,0:T(8,128)S(1)} all-to-all(f32[16,32,128]{2,1,0:T(8,128)S(1)} %get-tuple-element.28), channel_id=1, replica_groups=mesh['rep'=2,'gx'=16] {'gx'}, dimensions={0} | all-to-all | bytes 524288 | tf_op jit(solution)/shard_map/all_to_all | solution.py:853
  150.3 0.8 finish.1
  (39 shorter events, 1.7 us)
Async XLA Ops:
  0.6 12.1 %copy-start = (f32[128,128]{1,0:T(8,128)S(1)}, f32[128,128]{1,0:T(8,128)}, u32[]{:S(2)}) copy-start(f32[128,128]{1,0:T(8,128)} %constant.71.clone.refs_1_) | copy-start | bytes 196612
  3.8 19.6 %all-to-all-start = ((f32[16,48,128]{2,1,0:T(8,128)}), f32[16,48,128]{2,1,0:T(8,128)S(1)}, u32[]{:S(2)}, u32[]{:S(2)}) async-start(f32[16,48,128]{2,1,0:T(8,128)} %get-tuple-element.16), calls=%async_computation | async-start | bytes 786432 | tf_op jit(solution)/shard_map/all_to_all | solution.py:853
  14.5 35.8 %copy-start.1 = (f32[3,1024]{1,0:T(4,128)S(1)}, f32[3,1024]{1,0:T(4,128)}, u32[]{:S(2)}) copy-start(f32[3,1024]{1,0:T(4,128)} %refs_10_.1) | copy-start | bytes 36868
  46.8 21.2 %all-to-all-start.1 = ((f32[16,24,128]{2,1,0:T(8,128)}), f32[16,24,128]{2,1,0:T(8,128)S(1)}, u32[]{:S(2)}, u32[]{:S(2)}) async-start(f32[16,24,128]{2,1,0:T(8,128)} %get-tuple-element.18), calls=%async_computation.1 | async-start | bytes 393216 | tf_op jit(solution)/shard_map/all_to_all | solution.py:853
  50.3 5.7 %collective-permute-start.1 = (f32[3,384]{1,0:T(4,128)S(1)}, f32[3,384]{1,0:T(4,128)S(1)}, u32[]{:S(2)}, u32[]{:S(2)}) collective-permute-start(f32[3,384]{1,0:T(4,128)S(1)} %get-tuple-element.30), channel_id=1, source_target_pairs={{1,0},{2,1},{3,2},{4,3},{5,4},{6,5},{7,6},{8,7},{9,8},{10,9},{11,1... | collective-permute-start | bytes 13832 | tf_op jit(solution)/shard_map/ppermute | solution.py:871
  54.7 5.8 %collective-permute-start = (f32[3,384]{1,0:T(4,128)S(1)}, f32[3,384]{1,0:T(4,128)S(1)}, u32[]{:S(2)}, u32[]{:S(2)}) collective-permute-start(f32[3,384]{1,0:T(4,128)S(1)} %get-tuple-element.31), channel_id=1, source_target_pairs={{0,1},{1,2},{2,3},{3,4},{4,5},{5,6},{6,7},{7,8},{8,9},{9,10},{10,1... | collective-permute-start | bytes 13832 | tf_op jit(solution)/shard_map/ppermute | solution.py:870
  56.0 4.4 %copy-start.2 = (f32[3,384]{1,0:T(4,128)}, f32[3,384]{1,0:T(4,128)S(1)}, u32[]{:S(2)}) copy-start(f32[3,384]{1,0:T(4,128)S(1)} %collective-permute-done.1.right_ref.refs_11_) | copy-start | bytes 13828
  60.4 0.6 copy-start.3
  93.7 12.5 %all-to-all-start.3 = ((f32[16,24,128]{2,1,0:T(8,128)}), f32[16,24,128]{2,1,0:T(8,128)S(1)}, u32[]{:S(2)}, u32[]{:S(2)}) async-start(f32[16,24,128]{2,1,0:T(8,128)} %field.4), calls=%async_computation.3 | async-start | bytes 393216 | tf_op jit(solution)/shard_map/all_to_all | solution.py:853
  97.3 14.3 %copy-start.4 = (s32[8,7]{1,0:T(8,128)S(1)}, s32[8,7]{1,0:T(8,128)}, u32[]{:S(2)}) copy-start(s32[8,7]{1,0:T(8,128)} %list_ref.3) | copy-start | bytes 676
  97.3 14.4 %copy-start.5 = (s32[8]{0:T(128)S(1)}, s32[8]{0:T(128)}, u32[]{:S(2)}) copy-start(s32[8]{0:T(128)} %count_ref.3) | copy-start | bytes 100
  106.9 13.6 %all-to-all-start.4 = ((f32[16,24,128]{2,1,0:T(8,128)}), f32[16,24,128]{2,1,0:T(8,128)S(1)}, u32[]{:S(2)}, u32[]{:S(2)}) async-start(f32[16,24,128]{2,1,0:T(8,128)} %get-tuple-element.24), calls=%async_computation.4 | async-start | bytes 393216 | tf_op jit(solution)/shard_map/all_to_all | solution.py:853

commit v4 on v3

--- a/solution.py
+++ b/solution.py
@@ -417,24 +417,17 @@
 
 
 def near_tiles(refs, vec_ref, near_ref, col_ref):
-    rank_ref, left_ref, pos_ref, right_ref = refs
-    blocks = pos_ref.shape[1] // TILE
+    rank_ref, pos_ref = refs
+    blocks = pos_ref.shape[1] // TILE - 2 * HALO_BLK
     total = vec_ref.shape[0] * blocks
-    shift = 1.0 * blocks
     for j in range(blocks + 2 * HALO_BLK):
         i = j - HALO_BLK
         g = rank_ref[0] * blocks + i
         if i < 0:
             g = jnp.where(g < 0, g + total, g)
-            source, i, move = left_ref, j, -shift
-        elif i < blocks:
-            source, move = pos_ref, 0.0
-        else:
+        elif i >= blocks:
             g = jnp.where(g >= total, g - total, g)
-            source, i, move = right_ref, i - blocks, shift
-        rows = source[:, i * TILE : (i + 1) * TILE]
-        near_ref[j, 0:1, :] = rows[0:1] + move
-        near_ref[j, 1:3, :] = rows[1:3]
+        near_ref[j, 0:3, :] = pos_ref[:, j * TILE : (j + 1) * TILE]
         src = lax.shift_right_logical(g, 3)
         block = g & (ROWS - 1)
         for c in range(3):
@@ -467,7 +460,8 @@
             third = wts_ref[b * SPAN + e] * (inverse * square)
             if e == HALO_BLK:
                 third = jnp.where(ahead == start - b * TILE, 0.0, third)
-            fifth = (third * square) * (3.0 * (dx * vx + dy * vy + dz * vz))
+            wx, wy, wz = 3.0 * vx, 3.0 * vy, 3.0 * vz
+            fifth = (third * square) * (dx * wx + dy * wy + dz * wz)
             sx = sx + (third * vx - fifth * dx)
             sy = sy + (third * vy - fifth * dy)
             sz = sz + (third * vz - fifth * dz)
@@ -489,17 +483,17 @@
 
 def field_kernel(mode, *refs):
     making, closing = mode
-    v_ref, rows_ref, cols_ref, kern_hbm, *refs = refs
+    v_ref, rows_ref, cols_ref, kern_ref, *refs = refs
     if making:
         z_ref, turn_ref, out_ref, tab_hbm, yt_hbm, *refs = refs
         atom_ref = v_ref
     elif closing:
         atom_ref, tab_hbm, yt_hbm, wts_ref, *refs = refs
-        places, known, refs = refs[:4], refs[4:8], refs[8:]
+        places, known, refs = refs[:2], refs[2:6], refs[6:]
         out_ref, pair_ref, *refs = refs
     else:
         atom_ref, tab_hbm, yt_hbm, out_ref, *refs = refs
-    tab, sem, yt_ref, yt_sem, kern_ref, kern_sem, grid_ref, *refs = refs
+    tab, sem, yt_ref, yt_sem, grid_ref, *refs = refs
     parts = out_ref.shape[0]
     grid = rows_ref.shape[0]
     blocks = tab.shape[0] // parts
@@ -516,12 +510,10 @@
             pltpu.make_async_copy(ends[1][0], ends[1][1], sem.at[s]),
         ]
 
-    kern_copy = pltpu.make_async_copy(kern_hbm, kern_ref, kern_sem)
     if not making:
         for s in range(parts):
             for copy in table_copies(s):
                 copy.start()
-    kern_copy.start()
     grid_ref[...] = jnp.zeros(grid_ref.shape, F32)
     if making:
         make_tables = table_maker(atom_ref, z_ref, turn_ref, tab, yt_ref)
@@ -594,7 +586,6 @@
         [jnp.where(lower, folded(j), folded(j + ROWS)) for j in range(ROWS)], axis=1
     )
     spectrum = product(rows_ref[...], charge)
-    kern_copy.wait()
     weighted = spectrum * kern_ref[...]
     potential = product(cols_ref[...], weighted)
     for j in range(ROWS):
@@ -659,8 +650,9 @@
     tab_shape = jax.ShapeDtypeStruct((grid, grid, 2 * TILE), BF16)
     yt_shape = jax.ShapeDtypeStruct((grid, 2 * LINES, TILE), F32)
     tables = [near(tables[0]), *tables[1:]] if tables else []
-    args = [near(vec), rows, cols, kern, *first, *tables, *final[:5], *map(near, final[5:])]
-    specs = [IN_VMEM] * 3 + [IN_HBM] + [IN_VMEM] * len(first)
+    first = [near(x) for x in first]
+    args = [near(vec), near(rows), near(cols), near(kern), *first, *tables, *final[:2], *map(near, final[2:])]
+    specs = [IN_VMEM] * (4 + len(first))
     if tables:
         specs += [IN_VMEM, IN_HBM, IN_HBM]
     if final:
@@ -673,8 +665,6 @@
         pltpu.SemaphoreType.DMA((parts,)),
         pltpu.VMEM(yt_shape.shape, F32),
         pltpu.SemaphoreType.DMA((parts,)),
-        pltpu.VMEM(kern.shape, F32),
-        pltpu.SemaphoreType.DMA(()),
         pltpu.VMEM(((grid + REACH) * LINES, grid), F32),
     ]
     if first:
@@ -699,9 +689,9 @@
     )(*args)
 
 
-def pair_kernel(list_ref, count_ref, rank_ref, left_ref, pos_ref, right_ref, vec_ref, out_ref, acc_ref, near_ref, col_ref):
-    blocks = pos_ref.shape[1] // TILE
-    near_tiles((rank_ref, left_ref, pos_ref, right_ref), vec_ref, near_ref, col_ref)
+def pair_kernel(list_ref, count_ref, rank_ref, pos_ref, vec_ref, out_ref, acc_ref, near_ref, col_ref):
+    blocks = out_ref.shape[0] // 3
+    near_tiles((rank_ref, pos_ref), vec_ref, near_ref, col_ref)
     chunk = TILE // 2
     shape = (chunk, TILE)
     ahead = lax.broadcasted_iota(jnp.int32, shape, 1) - lax.broadcasted_iota(jnp.int32, shape, 0)
@@ -719,11 +709,12 @@
                 tile = near_ref[j]
                 dx, dy, dz = hx - tile[0:1], hy - tile[1:2], hz - tile[2:3]
                 vx, vy, vz = tile[3:4], tile[4:5], tile[5:6]
+                wx, wy, wz = 3.0 * vx, 3.0 * vy, 3.0 * vz
                 inverse = lax.rsqrt(dx * dx + dy * dy + dz * dz + 1.0)
                 square = inverse * inverse
                 itself = ahead == c * chunk - (j - b - HALO_BLK) * TILE
                 third = jnp.where(itself, 0.0, inverse * square)
-                fifth = (third * square) * (3.0 * (dx * vx + dy * vy + dz * vz))
+                fifth = (third * square) * (dx * wx + dy * wy + dz * wz)
                 return (
                     sx + (third * vx - fifth * dx),
                     sy + (third * vy - fifth * dy),
@@ -742,11 +733,11 @@
 
 
 def pair_call(tiles, counts, places, vec):
-    rank, left, pos, right = places
-    blocks = pos.shape[1] // TILE
+    rank, pos = places
+    blocks = pos.shape[1] // TILE - 2 * HALO_BLK
     return pl.pallas_call(
         pair_kernel,
-        in_specs=[IN_SMEM] * 3 + [IN_VMEM] * 4,
+        in_specs=[IN_SMEM] * 3 + [IN_VMEM] * 2,
         out_specs=IN_VMEM,
         out_shape=pltpu.VMEM((3 * blocks, TILE), F32),
         scratch_shapes=[
@@ -756,7 +747,7 @@
         ],
         name="pair",
         **params(1 << 30),
-    )(tiles, counts, rank, left, pos, right, near(vec))
+    )(tiles, counts, rank, near(pos), near(vec))
 
 
 def update_kernel(ret_ref, pair_ref, inv_ref, own_ref, out_ref):
@@ -866,9 +857,10 @@
         field, inv_polar[None, :], x_spline.transpose(1, 0, 2), yz_spline, parts
     )
     everyone = swap(packed)
-    edges, everyone = lax.optimization_barrier((positions, everyone))
-    left = lax.ppermute(edges[:, atoms - halo :], "gx", up)
-    right = lax.ppermute(edges[:, :halo], "gx", down)
+    left = lax.ppermute(positions[:, atoms - halo :], "gx", up)
+    right = lax.ppermute(positions[:, :halo], "gx", down)
+    shift = jnp.where(jnp.arange(3) == 0, 1.0 * blocks, 0.0)[:, None]
+    joined = jnp.concatenate([left - shift, positions, right + shift], axis=1)
 
     offsets = jnp.arange(SPAN, dtype=jnp.int32)
     block_ids = jnp.arange(blocks, dtype=jnp.int32)
@@ -908,7 +900,7 @@
 
     partial, table, yt = field_call(everyone, rows, cols, kern, first=(z_rows, turns))
     tables = (everyone, table, yt)
-    places = (rank[None].astype(jnp.int32), left, positions, right)
+    places = (rank[None].astype(jnp.int32), joined)
     vec, vectors = everyone, [own]
     for step in range(ITERS):
         last = step + 1 == ITERS

time: 152 us -> 145 us (0.954)
  Pallas kernels: 73.4 us -> 70.8 us
  starting transfers between devices: 23.4 us -> 20.8 us
  waiting for transfers between devices: 24.7 us -> 22.9 us
  blocking collectives: 24.2 us -> 25.9 us
    ppermute x2, waiting for transfers between devices: 5.75 us -> 0.01 us  [the longest x1 0.01 us: per_device_modes(): right = lax.ppermute(positions[:, :halo], 'gx', down)]
    all_to_all x4, waiting for transfers between devices: 18.9 us -> 22.9 us  [swap(): return lax.all_to_all(x, 'gx', split_axis=0, concat_axis=0, tiled=True)]
    all_to_all x4, starting transfers between devices: 19.1 us -> 15.3 us  [swap(): return lax.all_to_all(x, 'gx', split_axis=0, concat_axis=0, tiled=True)]
    pallas_call x3, Pallas kernels: 54.8 us -> 52.4 us  [field_call(): pl.pallas_call(lambda *refs: field_kernel(mode, *refs), in_specs=specs, o...]
    all_to_all x2, blocking collectives: 24.2 us -> 25.9 us  [swap(): return lax.all_to_all(x, 'gx', split_axis=0, concat_axis=0, tiled=True)]
  transfers between devices with their start and end apart: 6 -> 6, of which waited for: 5 -> 4; matrix products, arithmetic and copies ran while one was open for 3% -> 1% of each run, Pallas kernels for 9% -> 27%
where the time goes in v4:
time: 145 us; the launch traced here: 144 us
  Pallas kernels  70.8 us (49%)
  blocking collectives  25.9 us (18%)
  waiting for transfers between devices  22.9 us (16%)
  starting transfers between devices  20.8 us (14%)
  local copies, waits for them, and re-layouts  2.1 us (1%)
    pallas_call x3, Pallas kernels, field_call(): pl.pallas_call(lambda *refs: field_kernel(mode, *refs), in_specs=specs, o...  52.4 us
    all_to_all x2, blocking collectives, swap(): return lax.all_to_all(x, 'gx', split_axis=0, concat_axis=0, tiled=True)  25.9 us
    all_to_all x4, waiting for transfers between devices, swap(): return lax.all_to_all(x, 'gx', split_axis=0, concat_axis=0, tiled=True)  22.9 us
    all_to_all x4, starting transfers between devices, swap(): return lax.all_to_all(x, 'gx', split_axis=0, concat_axis=0, tiled=True)  15.3 us
    pallas_call x2, Pallas kernels, pair_call(): pl.pallas_call(pair_kernel, in_specs=[IN_SMEM] * 3 + [IN_VMEM] * 2, out_s...  13.7 us
    ppermute x1, starting transfers between devices, per_device_modes(): right = lax.ppermute(positions[:, :halo], 'gx', down)  4.95 us
    pallas_call x1, Pallas kernels, pack_call(): pl.pallas_call(pack_kernel, in_specs=[IN_VMEM] * 4, out_specs=[IN_VMEM] *...  3.1 us
  transfers between devices with their start and end apart: 6, of which 4 were waited for; matrix products, arithmetic and copies ran while one was open for 1% of the time, Pallas kernels for 27%

profile of v4, /device:TPU:0, one launch (start us, length us, event | category | flops | bytes accessed | tf_op | source)
XLA Modules:
  0.0 144.2 jit_solution(269910254098161840)
XLA Ops:
  0.7 0.8 fusion.17
  1.4 0.5 collective-permute-start
  1.9 5.0 %collective-permute-start.1 = (f32[3,384]{1,0:T(4,128)S(1)}, f32[3,384]{1,0:T(4,128)S(1)}, u32[]{:S(2)}, u32[]{:S(2)}) collective-permute-start(f32[3,384]{1,0:T(4,128)S(1)} %get-tuple-element.27), channel_id=1, source_target_pairs={{1,0},{2,1},{3,2},{4,3},{5,4},{6,5},{7,6},{8,7},{9,8},{10,9},{11,1... | collective-permute-start | bytes 13832 | tf_op jit(solution)/shard_map/ppermute | solution.py:861
  6.9 3.1 %pack.1 = (f32[24,128]{1,0:T(8,128)S(1)}, f32[8,128]{1,0:T(8,128)S(1)}, f32[16,48,128]{2,1,0:T(8,128)}) custom-call(f32[3,1024]{1,0:T(4,128)} %field_ref.1, f32[1,1024]{1,0:T(1,128)} %bitcast.14, f32[5,2,1024]{2,1,0:T(2,128)} %bitcast.13, f32[4,1024,128]{2,1,0:T(8,128)} %yz_ref.1), custom_call_target="tpu_custom_call" | custom-call | flops 67108864 | bytes 4194304 | tf_op jit(solution)/shard_map/pack/pallas_call | solution.py:338
  9.9 3.7 %all-to-all-start = ((f32[16,48,128]{2,1,0:T(8,128)}), f32[16,48,128]{2,1,0:T(8,128)S(1)}, u32[]{:S(2)}, u32[]{:S(2)}) async-start(f32[16,48,128]{2,1,0:T(8,128)} %get-tuple-element.14), calls=%async_computation | async-start | bytes 786432 | tf_op jit(solution)/shard_map/all_to_all | solution.py:844
  13.7 0.1 fusion.5
  14.7 0.3 fusion.2.refs_3_
  15.0 10.8 %all-to-all-done.refs_0_.vec_ref.refs_4_ = f32[16,48,128]{2,1,0:T(8,128)S(1)} async-done(((f32[16,48,128]{2,1,0:T(8,128)}), f32[16,48,128]{2,1,0:T(8,128)S(1)}, u32[]{:S(2)}, u32[]{:S(2)}) %all-to-all-start) | async-done | bytes 393248 | tf_op jit(solution)/shard_map/all_to_all | solution.py:844
  25.8 22.4 %field.3 = (f32[16,24,128]{2,1,0:T(8,128)}, bf16[128,128,256]{2,1,0:T(8,128)(2,1)}, f32[128,32,128]{2,1,0:T(8,128)}) custom-call(f32[16,48,128]{2,1,0:T(8,128)S(1)} %all-to-all-done.refs_0_.vec_ref.refs_4_, f32[128,128]{1,0:T(8,128)S(1)} %copy-done, f32[128,128]{1,0:T(8,128)S(1)} %copy-done.1, f32[128,1024]{1,0:T(8,128)S(1)} %fusion.2.refs_3_, ...), custom_call_target="tpu_custom_call" | custom-call | flops 2147483648 | bytes 4194304 | tf_op jit(solution)/shard_map/field/pallas_call | solution.py:681
  48.3 3.5 %all-to-all-start.1 = ((f32[16,24,128]{2,1,0:T(8,128)}), f32[16,24,128]{2,1,0:T(8,128)S(1)}, u32[]{:S(2)}, u32[]{:S(2)}) async-start(f32[16,24,128]{2,1,0:T(8,128)} %get-tuple-element.15), calls=%async_computation.1 | async-start | bytes 393216 | tf_op jit(solution)/shard_map/all_to_all | solution.py:844
  51.9 6.8 %pair.2.pair_ref = f32[24,128]{1,0:T(8,128)S(1)} custom-call(s32[8,7]{1,0:T(8,128)} %list_ref.3, s32[8]{0:T(128)} %count_ref.3, s32[1]{0:T(128)} %bitcast.7.rank_ref.refs_8_, f32[3,1792]{1,0:T(4,128)S(1)} %pad_maximum_fusion.pos_ref.refs_9_, f32[16,48,128]{2,1,0:T(8,128)S(1)} %all-to-all-done.refs_0_.vec_ref.refs_4_), custom_call_target="tpu_custom_call" | custom-call | flops 1073741824 | bytes 4194304 | tf_op jit(solution)/shard_map/pair/pallas_call | solution.py:738
  58.7 2.0 %all-to-all-done.1.ret_ref = f32[16,24,128]{2,1,0:T(8,128)S(1)} async-done(((f32[16,24,128]{2,1,0:T(8,128)}), f32[16,24,128]{2,1,0:T(8,128)S(1)}, u32[]{:S(2)}, u32[]{:S(2)}) %all-to-all-start.1) | async-done | bytes 196640 | tf_op jit(solution)/shard_map/all_to_all | solution.py:844
  60.8 13.3 %all_to_all.30.refs_0_.vec_ref = f32[16,24,128]{2,1,0:T(8,128)S(1)} all-to-all(f32[16,24,128]{2,1,0:T(8,128)S(1)} %get-tuple-element.17), channel_id=1, replica_groups=mesh['rep'=2,'gx'=16] {'gx'}, dimensions={0} | all-to-all | bytes 393216 | tf_op jit(solution)/shard_map/all_to_all | solution.py:844
  74.1 13.2 %field.4 = f32[16,24,128]{2,1,0:T(8,128)} custom-call(f32[16,24,128]{2,1,0:T(8,128)S(1)} %all_to_all.30.refs_0_.vec_ref, f32[128,128]{1,0:T(8,128)S(1)} %copy-done, f32[128,128]{1,0:T(8,128)S(1)} %copy-done.1, f32[128,1024]{1,0:T(8,128)S(1)} %fusion.2.refs_3_, f32[16,48,128]{2,1,0:T(8,128)S(1)} %all-to-all-done.refs_0_.vec_ref.refs_4_, ...), custom_call_target="tpu_custom_call" | custom-call | flops 2147483648 | bytes 4194304 | tf_op jit(solution)/shard_map/field/pallas_call | solution.py:681
  87.2 3.5 %all-to-all-start.3 = ((f32[16,24,128]{2,1,0:T(8,128)}), f32[16,24,128]{2,1,0:T(8,128)S(1)}, u32[]{:S(2)}, u32[]{:S(2)}) async-start(f32[16,24,128]{2,1,0:T(8,128)} %field.4), calls=%async_computation.3 | async-start | bytes 393216 | tf_op jit(solution)/shard_map/all_to_all | solution.py:844
  90.8 6.9 %pair.3.pair_ref = f32[24,128]{1,0:T(8,128)S(1)} custom-call(s32[8,7]{1,0:T(8,128)} %list_ref.3, s32[8]{0:T(128)} %count_ref.3, s32[1]{0:T(128)} %bitcast.7.rank_ref.refs_8_, f32[3,1792]{1,0:T(4,128)S(1)} %pad_maximum_fusion.pos_ref.refs_9_, f32[16,24,128]{2,1,0:T(8,128)S(1)} %all_to_all.30.refs_0_.vec_ref), custom_call_target="tpu_custom_call" | custom-call | flops 1073741824 | bytes 4194304 | tf_op jit(solution)/shard_map/pair/pallas_call | solution.py:738
  97.7 2.0 %all-to-all-done.3.ret_ref = f32[16,24,128]{2,1,0:T(8,128)S(1)} async-done(((f32[16,24,128]{2,1,0:T(8,128)}), f32[16,24,128]{2,1,0:T(8,128)S(1)}, u32[]{:S(2)}, u32[]{:S(2)}) %all-to-all-start.3) | async-done | bytes 196640 | tf_op jit(solution)/shard_map/all_to_all | solution.py:844
  99.7 0.7 update.3
  100.4 4.6 %all-to-all-start.4 = ((f32[16,24,128]{2,1,0:T(8,128)}), f32[16,24,128]{2,1,0:T(8,128)S(1)}, u32[]{:S(2)}, u32[]{:S(2)}) async-start(f32[16,24,128]{2,1,0:T(8,128)} %get-tuple-element.20), calls=%async_computation.4 | async-start | bytes 393216 | tf_op jit(solution)/shard_map/all_to_all | solution.py:844
  105.2 0.6 reshape.195.refs_7_
  105.8 8.2 %all-to-all-done.4.refs_0_ = f32[16,24,128]{2,1,0:T(8,128)S(1)} async-done(((f32[16,24,128]{2,1,0:T(8,128)}), f32[16,24,128]{2,1,0:T(8,128)S(1)}, u32[]{:S(2)}, u32[]{:S(2)}) %all-to-all-start.4) | async-done | bytes 196640 | tf_op jit(solution)/shard_map/all_to_all | solution.py:844
  114.0 16.8 %field.5 = (f32[16,32,128]{2,1,0:T(8,128)S(1)}, f32[24,128]{1,0:T(8,128)S(1)}) custom-call(f32[16,24,128]{2,1,0:T(8,128)S(1)} %all-to-all-done.4.refs_0_, f32[128,128]{1,0:T(8,128)S(1)} %copy-done, f32[128,128]{1,0:T(8,128)S(1)} %copy-done.1, f32[128,1024]{1,0:T(8,128)S(1)} %fusion.2.refs_3_, f32[16,48,128]{2,1,0:T(8,128)S(1)} %all-to-all-done.refs_0_.vec_ref.refs_4_, ...), custom_call_target="tpu_custom_call" | custom-call | flops 2147483648 | bytes 4194304 | tf_op jit(solution)/shard_map/field/pallas_call | solution.py:681
  130.8 12.6 %all_to_all.31.ret_ref = f32[16,32,128]{2,1,0:T(8,128)S(1)} all-to-all(f32[16,32,128]{2,1,0:T(8,128)S(1)} %get-tuple-element.24), channel_id=1, replica_groups=mesh['rep'=2,'gx'=16] {'gx'}, dimensions={0} | all-to-all | bytes 524288 | tf_op jit(solution)/shard_map/all_to_all | solution.py:844
  143.4 0.8 finish.1
  (40 shorter events, 1.1 us)
Async XLA Ops:
  0.6 14.0 %copy-start = (f32[128,128]{1,0:T(8,128)S(1)}, f32[128,128]{1,0:T(8,128)}, u32[]{:S(2)}) copy-start(f32[128,128]{1,0:T(8,128)} %constant.74.clone.refs_1_) | copy-start | bytes 196612
  0.6 25.2 %copy-start.1 = (f32[128,128]{1,0:T(8,128)S(1)}, f32[128,128]{1,0:T(8,128)}, u32[]{:S(2)}) copy-start(f32[128,128]{1,0:T(8,128)} %constant.75.clone.refs_2_) | copy-start | bytes 196612
  1.4 50.4 %collective-permute-start = (f32[3,384]{1,0:T(4,128)S(1)}, f32[3,384]{1,0:T(4,128)S(1)}, u32[]{:S(2)}, u32[]{:S(2)}) collective-permute-start(f32[3,384]{1,0:T(4,128)S(1)} %get-tuple-element.26), channel_id=1, source_target_pairs={{0,1},{1,2},{2,3},{3,4},{4,5},{5,6},{6,7},{7,8},{8,9},{9,10},{10,1... | collective-permute-start | bytes 13832 | tf_op jit(solution)/shard_map/ppermute | solution.py:860
  1.9 49.9 %collective-permute-start.1 = (f32[3,384]{1,0:T(4,128)S(1)}, f32[3,384]{1,0:T(4,128)S(1)}, u32[]{:S(2)}, u32[]{:S(2)}) collective-permute-start(f32[3,384]{1,0:T(4,128)S(1)} %get-tuple-element.27), channel_id=1, source_target_pairs={{1,0},{2,1},{3,2},{4,3},{5,4},{6,5},{7,6},{8,7},{9,8},{10,9},{11,1... | collective-permute-start | bytes 13832 | tf_op jit(solution)/shard_map/ppermute | solution.py:861
  9.9 15.9 %all-to-all-start = ((f32[16,48,128]{2,1,0:T(8,128)}), f32[16,48,128]{2,1,0:T(8,128)S(1)}, u32[]{:S(2)}, u32[]{:S(2)}) async-start(f32[16,48,128]{2,1,0:T(8,128)} %get-tuple-element.14), calls=%async_computation | async-start | bytes 786432 | tf_op jit(solution)/shard_map/all_to_all | solution.py:844
  15.0 36.9 %copy-start.2 = (f32[3,1024]{1,0:T(4,128)S(1)}, f32[3,1024]{1,0:T(4,128)}, u32[]{:S(2)}) copy-start(f32[3,1024]{1,0:T(4,128)} %param.9) | copy-start | bytes 36868
  48.3 12.5 %all-to-all-start.1 = ((f32[16,24,128]{2,1,0:T(8,128)}), f32[16,24,128]{2,1,0:T(8,128)S(1)}, u32[]{:S(2)}, u32[]{:S(2)}) async-start(f32[16,24,128]{2,1,0:T(8,128)} %get-tuple-element.15), calls=%async_computation.1 | async-start | bytes 393216 | tf_op jit(solution)/shard_map/all_to_all | solution.py:844
  87.2 12.5 %all-to-all-start.3 = ((f32[16,24,128]{2,1,0:T(8,128)}), f32[16,24,128]{2,1,0:T(8,128)S(1)}, u32[]{:S(2)}, u32[]{:S(2)}) async-start(f32[16,24,128]{2,1,0:T(8,128)} %field.4), calls=%async_computation.3 | async-start | bytes 393216 | tf_op jit(solution)/shard_map/all_to_all | solution.py:844
  90.8 14.2 %copy-start.3 = (s32[8,7]{1,0:T(8,128)S(1)}, s32[8,7]{1,0:T(8,128)}, u32[]{:S(2)}) copy-start(s32[8,7]{1,0:T(8,128)} %list_ref.3) | copy-start | bytes 676
  90.8 14.3 %copy-start.4 = (s32[8]{0:T(128)S(1)}, s32[8]{0:T(128)}, u32[]{:S(2)}) copy-start(s32[8]{0:T(128)} %count_ref.3) | copy-start | bytes 100
  100.4 13.6 %all-to-all-start.4 = ((f32[16,24,128]{2,1,0:T(8,128)}), f32[16,24,128]{2,1,0:T(8,128)S(1)}, u32[]{:S(2)}, u32[]{:S(2)}) async-start(f32[16,24,128]{2,1,0:T(8,128)} %get-tuple-element.20), calls=%async_computation.4 | async-start | bytes 393216 | tf_op jit(solution)/shard_map/all_to_all | solution.py:844
